TPU v7x, 512 devices: a whole 4x8x8 slice. The times are simulated.
512 devices in a mesh: gx: 32 (over z, y_hi), gy: 16 (over y_lo, x, core).
Axes of the slice: x: 4, y: 8 (y_hi: 4, y_lo: 2; y = y_hi * 2 + y_lo), z: 8, core: 2. Of those that a mesh axis runs over, the one named last changes fastest.
Arguments:
- scalars: float32 [20, 256, 256, 128], P(None, 'gx', 'gy'), may hold values from -6 to 6
- velocity: float32 [3, 256, 256, 128], P(None, 'gx', 'gy'), may hold values from -4 to 4
- diffusivity: float32 [256, 256, 128], P('gx', 'gy'), may hold values from 0.05 to 0.6
- burn_list: int32 [32, 16, 64], P('gx', 'gy'), may hold values from 0 to 128, as said below
- w_in: bfloat16 [800, 20], replicated, may hold values from -1.25 to 1.25
- w_mid: bfloat16 [400, 800], replicated, may hold values from -0.21875 to 0.21875
- w_out: bfloat16 [20, 400], replicated, may hold values from -0.3125 to 0.3125
Outputs:
- scalars_out: float32 [20, 256, 256, 128], P(None, 'gx', 'gy')
- velocity_out: float32 [3, 256, 256, 128], P(None, 'gx', 'gy')
Inputs may be any that keep to these rules, and one draw needn't show every extreme that they name: `burn_list`: in each device's list the burning columns come first, distinct, and the remaining slots hold 128. A device lists 0 to 64 burning columns; in every group of devices with one gx index one device lists 64 and one lists none, and the group lists exactly 512 together.
All inputs are finite; a program needn't handle non-finite values.
Results may differ from a plain program's by a relative error of at most 0.0023.
Values may be sent and summed in bfloat16 or wider, within the bound.
No kernel may reach another device: no remote copies, remote signals or barrier semaphores. Data moves between devices by JAX's collectives and lax.ppermute only.
A program may use at most 64 MiB of HBM per device.

v0:
```python
import math

import jax
import jax.numpy as jnp
from jax import lax
from jax.sharding import PartitionSpec as P

time_step = 0.25


def padded_2(value, sides, width):
    edges = {}
    for axis, dim in sides:
        size, length = (lax.axis_size(axis), value.shape[dim])
        up = [(i, (i + 1) % size) for i in range(size)]
        last = lax.slice_in_dim(value, length - width, length, axis=dim)
        initial = lax.slice_in_dim(value, 0, width, axis=dim)
        edges[dim] = (
            lax.ppermute(last, axis, up),
            lax.ppermute(initial, axis, [(b, a) for a, b in up]),
        )
    done = []
    for _, dim in sides:
        low, high = edges[dim]
        around = [(width, width) if d in done else (0, 0) for d in range(value.ndim)]
        value = jnp.concatenate([jnp.pad(low, around), value, jnp.pad(high, around)], axis=dim)
        done.append(dim)
    return value


def hartley_table(length):
    position = jnp.arange(length, dtype=jnp.int32)
    product = position[:, None] * position[None, :] % length
    phase_angle = 2.0 * math.pi / length * product.astype(jnp.float32)
    return (jnp.cos(phase_angle) + jnp.sin(phase_angle)) / math.sqrt(length)


def cosine_table(length):
    position = jnp.arange(length, dtype=jnp.int32)
    product = position[:, None] * (2 * position[None, :] + 1) % (4 * length)
    phase_angle = math.pi / (2 * length) * product.astype(jnp.float32)
    weight = jnp.where(position == 0, math.sqrt(1.0 / length), math.sqrt(2.0 / length)).astype(
        jnp.float32
    )
    return weight[:, None] * jnp.cos(phase_angle)


def depth_next(values):
    return jnp.concatenate([values[..., 1:], values[..., -1:]], -1)


def depth_prev(values):
    return jnp.concatenate([values[..., :1], values[..., :-1]], -1)


def transport_rate(field_pad, flow_pad):
    center = field_pad[:, 1:-1, 1:-1]
    x_next = field_pad[:, 2:, 1:-1]
    x_prev = field_pad[:, :-2, 1:-1]
    y_next = field_pad[:, 1:-1, 2:]
    y_prev = field_pad[:, 1:-1, :-2]
    z_next = depth_next(center)
    z_prev = depth_prev(center)
    coefficient = flow_pad[3, 1:-1, 1:-1]
    advection = (
        flow_pad[0, 1:-1, 1:-1] * (x_next - x_prev) * 0.5
        + flow_pad[1, 1:-1, 1:-1] * (y_next - y_prev) * 0.5
        + flow_pad[2, 1:-1, 1:-1] * (z_next - z_prev) * 0.5
    )
    diffusion = 0.5 * (coefficient + flow_pad[3, 2:, 1:-1]) * (x_next - center) - 0.5 * (
        coefficient + flow_pad[3, :-2, 1:-1]
    ) * (center - x_prev)
    diffusion = (
        diffusion
        + 0.5 * (coefficient + flow_pad[3, 1:-1, 2:]) * (y_next - center)
        - 0.5 * (coefficient + flow_pad[3, 1:-1, :-2]) * (center - y_prev)
    )
    diffusion = (
        diffusion
        + 0.5 * (coefficient + depth_next(coefficient)) * (z_next - center)
        - 0.5 * (coefficient + depth_prev(coefficient)) * (center - z_prev)
    )
    return diffusion - advection


def network(blocks, w_in, w_mid, w_out):
    block_count = blocks.shape[0]
    bundle_size = 8
    padded_count = -(-block_count // bundle_size) * bundle_size

    def evaluate(bundle):
        hidden_one = jnp.einsum("hn,bnz->bhz", w_in, bundle, preferred_element_type=jnp.float32)
        hidden_one = jax.nn.gelu(hidden_one).astype(jnp.bfloat16)
        hidden_two = jnp.einsum(
            "kh,bhz->bkz", w_mid, hidden_one, preferred_element_type=jnp.float32
        )
        hidden_two = jax.nn.gelu(hidden_two).astype(jnp.bfloat16)
        return jnp.einsum("nk,bkz->bnz", w_out, hidden_two, preferred_element_type=jnp.float32)

    reaction = lax.map(
        evaluate, blocks.reshape((padded_count // bundle_size, bundle_size) + blocks.shape[1:])
    )
    return reaction.reshape((padded_count,) + reaction.shape[2:])


def solve_modes(spectrum, start_x, start_z, total_x, total_y, total_z):
    mode_x = start_x + jnp.arange(spectrum.shape[0], dtype=jnp.int32)
    mode_y = jnp.arange(spectrum.shape[1], dtype=jnp.int32)
    mode_z = start_z + jnp.arange(spectrum.shape[2], dtype=jnp.int32)
    eigen_x = 2.0 - 2.0 * jnp.cos(2.0 * math.pi / total_x * mode_x.astype(jnp.float32))
    eigen_y = 2.0 - 2.0 * jnp.cos(2.0 * math.pi / total_y * mode_y.astype(jnp.float32))
    eigen_z = 2.0 - 2.0 * jnp.cos(math.pi / total_z * mode_z.astype(jnp.float32))
    eigen = eigen_x[:, None, None] + eigen_y[None, :, None] + eigen_z[None, None, :]
    anchor = (
        (mode_x[:, None, None] == 0) & (mode_y[None, :, None] == 0) & (mode_z[None, None, :] == 0)
    ).astype(jnp.float32)
    return -spectrum * (1.0 - anchor) / (eigen + anchor)


def shards(scalars, velocity, diffusivity, burn_list, w_in, w_mid, w_out):
    channels = scalars.shape[0]
    joined = jnp.concatenate([scalars, velocity, diffusivity[None]], 0)
    padded = padded_2(joined.astype(jnp.bfloat16), (("gx", 1), ("gy", 2)), 1).astype(joined.dtype)
    field_pad = padded[:channels]
    inner_flow = padded[channels:]
    section_one = scalars + time_step * transport_rate(field_pad, inner_flow)
    section_pad = padded_2(section_one, (("gx", 1), ("gy", 2)), 1)
    transported = 0.5 * scalars + 0.5 * (
        section_one + time_step * transport_rate(section_pad, inner_flow)
    )
    divergence = 0.5 * (inner_flow[0, 2:, 1:-1] - inner_flow[0, :-2, 1:-1])
    divergence = divergence + 0.5 * (inner_flow[1, 1:-1, 2:] - inner_flow[1, 1:-1, :-2])
    vertical = inner_flow[2, 1:-1, 1:-1]
    divergence = divergence + 0.5 * (depth_next(vertical) - depth_prev(vertical))
    highest = lax.Precision.HIGHEST
    cells_x, cells_y, depth = divergence.shape
    total_x = cells_x * lax.axis_size("gx")
    total_y = cells_y * lax.axis_size("gy")
    table_x = hartley_table(total_x)
    table_y = hartley_table(total_y)
    table_z = cosine_table(depth)
    spectrum = jnp.einsum("az,xyz->xya", table_z, divergence, precision=highest)
    along_x = lax.all_to_all(spectrum, "gx", split_axis=2, concat_axis=0, tiled=True)
    along_x = jnp.einsum("cx,xyz->cyz", table_x, along_x, precision=highest)
    along_y = lax.all_to_all(
        along_x.astype(jnp.bfloat16), "gy", split_axis=0, concat_axis=1, tiled=True
    ).astype(along_x.dtype)
    along_y = jnp.einsum("by,xyz->xbz", table_y, along_y, precision=highest)
    solved = solve_modes(
        along_y,
        lax.axis_index("gy") * along_y.shape[0],
        lax.axis_index("gx") * along_y.shape[2],
        total_x,
        total_y,
        depth,
    )
    solved = jnp.einsum("by,xyz->xbz", table_y, solved, precision=highest)
    solved = lax.all_to_all(solved, "gy", split_axis=1, concat_axis=0, tiled=True)
    solved = jnp.einsum("cx,xyz->cyz", table_x, solved, precision=highest)
    solved = lax.all_to_all(solved, "gx", split_axis=0, concat_axis=2, tiled=True)
    pressure = jnp.einsum("az,xya->xyz", table_z, solved, precision=highest)
    pressure_pad = padded_2(pressure, (("gx", 0), ("gy", 1)), 1)
    grad_x = 0.5 * (pressure_pad[2:, 1:-1] - pressure_pad[:-2, 1:-1])
    grad_y = 0.5 * (pressure_pad[1:-1, 2:] - pressure_pad[1:-1, :-2])
    grad_z = 0.5 * (depth_next(pressure) - depth_prev(pressure))
    velocity_out = velocity - jnp.stack([grad_x, grad_y, grad_z])
    block_total = cells_x * cells_y
    flat_blocks = transported.reshape(channels, block_total, depth)
    listed = burn_list.reshape(-1)
    picked = jnp.take(flat_blocks, jnp.minimum(listed, block_total - 1), axis=1)
    chosen = jnp.transpose(picked, (1, 0, 2)).astype(jnp.bfloat16)
    own_rates = network(chosen, w_in, w_mid, w_out)
    updated = flat_blocks.at[:, listed].add(jnp.transpose(own_rates, (1, 0, 2)), mode="drop")
    scalars_out = updated.reshape(transported.shape)
    return (scalars_out, velocity_out)


def solution(mesh):
    in_specs = (
        P(None, "gx", "gy", None),
        P(None, "gx", "gy", None),
        P("gx", "gy", None),
        P("gx", "gy", None),
        P(),
        P(),
        P(),
    )
    out_specs = (P(None, "gx", "gy", None), P(None, "gx", "gy", None))
    return jax.shard_map(shards, mesh=mesh, in_specs=in_specs, out_specs=out_specs, check_vma=False)
```

profile of v0, /device:TPU:1, one launch (start us, length us, event | category | flops | bytes accessed | tf_op | source)
XLA Modules:
  0.0 168.3 jit_solution(7612224283811212633)
XLA Ops:
  2.4 4.5 %collective-permute-start = (bf16[24,8,1,128]{3,2,1,0:T(2,128)(2,1)S(1)}, bf16[24,8,1,128]{3,2,1,0:T(2,128)(2,1)S(1)}, u32[]{:S(2)}, u32[]{:S(2)}) collective-permute-start(bf16[24,8,1,128]{3,2,1,0:T(2,128)(2,1)S(1)} %get-tuple-element.76), channel_id=1, source_target_pairs={{0,1},{1,2},{2,3},{3,4},{4,5},{5,6},{6,7},{7,8},{8,9},{9,10},{10,1... | collective-permute-start | bytes 147464 | tf_op jit(solution)/shard_map/ppermute | solution.py:19
  6.9 4.2 %collective-permute-start.1 = (bf16[24,1,16,128]{3,2,1,0:T(8,128)(2,1)S(1)}, bf16[24,1,16,128]{3,2,1,0:T(8,128)(2,1)S(1)}, u32[]{:S(2)}, u32[]{:S(2)}) collective-permute-start(bf16[24,1,16,128]{3,2,1,0:T(8,128)(2,1)S(1)} %get-tuple-element.74), channel_id=1, source_target_pairs={{0,16},{16,32},{32,48},{48,64},{64,80},{80,96},{96,112},{112,128},... | collective-permute-start | bytes 294920 | tf_op jit(solution)/shard_map/ppermute | solution.py:19
  11.1 12.1 %collective-permute-start.2 = (bf16[24,1,16,128]{3,2,1,0:T(8,128)(2,1)S(1)}, bf16[24,1,16,128]{3,2,1,0:T(8,128)(2,1)S(1)}, u32[]{:S(2)}, u32[]{:S(2)}) collective-permute-start(bf16[24,1,16,128]{3,2,1,0:T(8,128)(2,1)S(1)} %get-tuple-element.75), channel_id=1, source_target_pairs={{16,0},{32,16},{48,32},{64,48},{80,64},{96,80},{112,96},{128,112},... | collective-permute-start | bytes 294920 | tf_op jit(solution)/shard_map/ppermute | solution.py:20
  43.9 6.8 %all-to-all-start = ((f32[32,1,512]{2,1,0:T(1,128)}), f32[32,1,512]{2,1,0:T(1,128)S(1)}, u32[]{:S(2)}, u32[]{:S(2)}) async-start(f32[32,1,512]{2,1,0:T(1,128)} %reshape.280), calls=%async_computation | async-start | bytes 131072 | tf_op jit(solution)/shard_map/all_to_all | solution.py:143
  50.7 7.5 %collective-permute-start.4 = (f32[20,1,16,128]{3,2,1,0:T(8,128)}, f32[20,1,16,128]{3,2,1,0:T(8,128)}, u32[]{:S(2)}, u32[]{:S(2)}) collective-permute-start(f32[20,1,16,128]{3,2,1,0:T(8,128)} %get-tuple-element.72), channel_id=1, source_target_pairs={{16,0},{32,16},{48,32},{64,48},{80,64},{96,80},{112,96},{128,112},... | collective-permute-start | bytes 491528 | tf_op jit(solution)/shard_map/ppermute | solution.py:20
  60.9 5.5 %collective-permute-start.6 = (f32[20,8,1,128]{3,2,1,0:T(1,128)}, f32[20,8,1,128]{3,2,1,0:T(1,128)}, u32[]{:S(2)}, u32[]{:S(2)}) collective-permute-start(f32[20,8,1,128]{3,2,1,0:T(1,128)} %get-tuple-element.66), channel_id=1, source_target_pairs={{1,0},{2,1},{3,2},{4,3},{5,4},{6,5},{7,6},{8,7},{9,8},{10,9},{11,1... | collective-permute-start | bytes 245768 | tf_op jit(solution)/shard_map/ppermute | solution.py:20
  70.6 3.4 %convolution_convert_fusion = bf16[256,16,4]{0,1,2:T(8,128)(2,1)} fusion(f32[32,8,16,4]{2,1,3,0:T(8,128)} %bitcast.183), kind=kOutput, calls=%fused_computation.81 | convolution fusion | flops 51396608 | bytes 98304 | tf_op jit(solution)/shard_map/cx,xyz->cyz/dot_general | solution.py:144
  75.8 5.5 %all-to-all-start.1 = ((bf16[16,2,512]{2,1,0:T(2,128)(2,1)}), bf16[16,2,512]{2,1,0:T(2,128)(2,1)S(1)}, u32[]{:S(2)}, u32[]{:S(2)}) async-start(bf16[16,2,512]{2,1,0:T(2,128)(2,1)} %reshape.282), calls=%async_computation.1 | async-start | bytes 65536 | tf_op jit(solution)/shard_map/all_to_all | solution.py:145
  81.4 4.1 %fusion.49 = f32[20,8,16,128]{3,2,1,0:T(8,128)S(1)} fusion(f32[20,8,16,128]{3,2,1,0:T(8,128)S(1)} %copy-done, f32[20,8,16,128]{3,2,1,0:T(8,128)S(1)} %multiply_add_fusion, f32[20,1,16,128]{3,2,1,0:T(8,128)} %collective-permute-done.5, f32[20,1,16,128]{3,2,1,0:T(8,128)} %collective-permute-done.4, f32[20,8,16,127]{3,2,1,0:T(8,128)} %get-tuple-element.69, ...), kind=kLoop, calls=%fused_computation.61 | loop fusion | flops 15400960 | bytes 7634944 | tf_op jit(solution)/shard_map/add | solution.py:128
  91.9 5.7 %all-to-all-start.2 = ((f32[16,1,1024]{2,1,0:T(1,128)}), f32[16,1,1024]{2,1,0:T(1,128)S(1)}, u32[]{:S(2)}, u32[]{:S(2)}) async-start(f32[16,1,1024]{2,1,0:T(1,128)} %reshape.284), calls=%async_computation.2 | async-start | bytes 131072 | tf_op jit(solution)/shard_map/all_to_all | solution.py:158
  98.5 4.9 %all-to-all-done.2 = f32[16,1,1024]{2,1,0:T(1,128)S(1)} async-done(((f32[16,1,1024]{2,1,0:T(1,128)}), f32[16,1,1024]{2,1,0:T(1,128)S(1)}, u32[]{:S(2)}, u32[]{:S(2)}) %all-to-all-start.2) | async-done | bytes 65568 | tf_op jit(solution)/shard_map/all_to_all | solution.py:158
  107.8 9.0 %all-to-all-start.3 = ((f32[32,1,512]{2,1,0:T(1,128)}), f32[32,1,512]{2,1,0:T(1,128)S(1)}, u32[]{:S(2)}, u32[]{:S(2)}) async-start(f32[32,1,512]{2,1,0:T(1,128)} %reshape.286), calls=%async_computation.3 | async-start | bytes 131072 | tf_op jit(solution)/shard_map/all_to_all | solution.py:160
  116.9 27.7 %while.10 = (s32[]{:T(128)}, f32[8,8,20,128]{3,2,1,0:T(8,128)S(1)}, bf16[8,8,20,128]{3,2,1,0:T(8,128)(2,1)}, bf16[800,20]{0,1:T(8,128)(2,1)S(1)}, bf16[400,800]{...) while((s32[]{:T(128)}, f32[8,8,20,128]{3,2,1,0:T(8,128)S(1)}, bf16[8,8,20,128]{3,2,1,0:T(8,128)(2,1)}, ...), condition=%wide.region_1.2_spmd, body=%wide.region_0.1_spmd.sunk | while | flops 715571200 | bytes 2559825 | solution.py:100
  116.9 3.2 %fusion.194 = bf16[8,400,128]{2,1,0:T(8,128)(2,1)S(1)} fusion(bf16[400,800]{1,0:T(8,128)(2,1)} %get-tuple-element.153, bf16[8,8,20,128]{3,2,1,0:T(8,128)(2,1)} %get-tuple-element.151, s32[]{:T(128)} %get-tuple-element.142, bf16[800,20]{0,1:T(8,128)(2,1)S(1)} %get-tuple-element.152), kind=kOutput, calls=%fused_computation.19.clone.1 | convolution fusion | flops 699187200 | bytes 1617664 | tf_op jit(solution)/shard_map/while/body/eval_jaxpr/kh,bhz->bkz/dot_general | solution.py:94
  120.3 3.2 %fusion.194 = bf16[8,400,128]{2,1,0:T(8,128)(2,1)S(1)} fusion(bf16[400,800]{1,0:T(8,128)(2,1)} %get-tuple-element.153, bf16[8,8,20,128]{3,2,1,0:T(8,128)(2,1)} %get-tuple-element.151, s32[]{:T(128)} %get-tuple-element.142, bf16[800,20]{0,1:T(8,128)(2,1)S(1)} %get-tuple-element.152), kind=kOutput, calls=%fused_computation.19.clone.1 | convolution fusion | flops 699187200 | bytes 1617664 | tf_op jit(solution)/shard_map/while/body/eval_jaxpr/kh,bhz->bkz/dot_general | solution.py:94
  123.8 3.2 %fusion.194 = bf16[8,400,128]{2,1,0:T(8,128)(2,1)S(1)} fusion(bf16[400,800]{1,0:T(8,128)(2,1)} %get-tuple-element.153, bf16[8,8,20,128]{3,2,1,0:T(8,128)(2,1)} %get-tuple-element.151, s32[]{:T(128)} %get-tuple-element.142, bf16[800,20]{0,1:T(8,128)(2,1)S(1)} %get-tuple-element.152), kind=kOutput, calls=%fused_computation.19.clone.1 | convolution fusion | flops 699187200 | bytes 1617664 | tf_op jit(solution)/shard_map/while/body/eval_jaxpr/kh,bhz->bkz/dot_general | solution.py:94
  127.2 3.2 %fusion.194 = bf16[8,400,128]{2,1,0:T(8,128)(2,1)S(1)} fusion(bf16[400,800]{1,0:T(8,128)(2,1)} %get-tuple-element.153, bf16[8,8,20,128]{3,2,1,0:T(8,128)(2,1)} %get-tuple-element.151, s32[]{:T(128)} %get-tuple-element.142, bf16[800,20]{0,1:T(8,128)(2,1)S(1)} %get-tuple-element.152), kind=kOutput, calls=%fused_computation.19.clone.1 | convolution fusion | flops 699187200 | bytes 1617664 | tf_op jit(solution)/shard_map/while/body/eval_jaxpr/kh,bhz->bkz/dot_general | solution.py:94
  130.7 3.2 %fusion.194 = bf16[8,400,128]{2,1,0:T(8,128)(2,1)S(1)} fusion(bf16[400,800]{1,0:T(8,128)(2,1)} %get-tuple-element.153, bf16[8,8,20,128]{3,2,1,0:T(8,128)(2,1)} %get-tuple-element.151, s32[]{:T(128)} %get-tuple-element.142, bf16[800,20]{0,1:T(8,128)(2,1)S(1)} %get-tuple-element.152), kind=kOutput, calls=%fused_computation.19.clone.1 | convolution fusion | flops 699187200 | bytes 1617664 | tf_op jit(solution)/shard_map/while/body/eval_jaxpr/kh,bhz->bkz/dot_general | solution.py:94
  134.2 3.2 %fusion.194 = bf16[8,400,128]{2,1,0:T(8,128)(2,1)S(1)} fusion(bf16[400,800]{1,0:T(8,128)(2,1)} %get-tuple-element.153, bf16[8,8,20,128]{3,2,1,0:T(8,128)(2,1)} %get-tuple-element.151, s32[]{:T(128)} %get-tuple-element.142, bf16[800,20]{0,1:T(8,128)(2,1)S(1)} %get-tuple-element.152), kind=kOutput, calls=%fused_computation.19.clone.1 | convolution fusion | flops 699187200 | bytes 1617664 | tf_op jit(solution)/shard_map/while/body/eval_jaxpr/kh,bhz->bkz/dot_general | solution.py:94
  137.6 3.2 %fusion.194 = bf16[8,400,128]{2,1,0:T(8,128)(2,1)S(1)} fusion(bf16[400,800]{1,0:T(8,128)(2,1)} %get-tuple-element.153, bf16[8,8,20,128]{3,2,1,0:T(8,128)(2,1)} %get-tuple-element.151, s32[]{:T(128)} %get-tuple-element.142, bf16[800,20]{0,1:T(8,128)(2,1)S(1)} %get-tuple-element.152), kind=kOutput, calls=%fused_computation.19.clone.1 | convolution fusion | flops 699187200 | bytes 1617664 | tf_op jit(solution)/shard_map/while/body/eval_jaxpr/kh,bhz->bkz/dot_general | solution.py:94
  141.1 3.2 %fusion.194 = bf16[8,400,128]{2,1,0:T(8,128)(2,1)S(1)} fusion(bf16[400,800]{1,0:T(8,128)(2,1)} %get-tuple-element.153, bf16[8,8,20,128]{3,2,1,0:T(8,128)(2,1)} %get-tuple-element.151, s32[]{:T(128)} %get-tuple-element.142, bf16[800,20]{0,1:T(8,128)(2,1)S(1)} %get-tuple-element.152), kind=kOutput, calls=%fused_computation.19.clone.1 | convolution fusion | flops 699187200 | bytes 1617664 | tf_op jit(solution)/shard_map/while/body/eval_jaxpr/kh,bhz->bkz/dot_general | solution.py:94
  144.6 3.1 %scatter_fusion = f32[20,128,128]{2,0,1:T(8,128)S(1)} fusion(f32[20,128,128]{2,0,1:T(8,128)S(1)} %copy.37, s32[64]{0:T(128)S(1)} %copy-done.20, f32[64,20,128]{2,1,0:T(8,128)S(1)} %bitcast.182), kind=kCustom, calls=%fused_computation.1 | custom fusion | flops 163840 | bytes 1966336 | tf_op jit(solution)/shard_map/scatter-add | solution.py:173
  151.7 7.2 %collective-permute-start.8 = (f32[1,16,128]{2,1,0:T(8,128)S(1)}, f32[1,16,128]{2,1,0:T(8,128)S(1)}, u32[]{:S(2)}, u32[]{:S(2)}) collective-permute-start(f32[1,16,128]{2,1,0:T(8,128)S(1)} %get-tuple-element.83), channel_id=1, source_target_pairs={{16,0},{32,16},{48,32},{64,48},{80,64},{96,80},{112,96},{128,112},... | collective-permute-start | bytes 24584 | tf_op jit(solution)/shard_map/ppermute | solution.py:20
  160.8 3.2 %collective-permute-start.10 = (f32[8,1,128]{2,1,0:T(1,128)S(1)}, f32[8,1,128]{2,1,0:T(1,128)S(1)}, u32[]{:S(2)}, u32[]{:S(2)}) collective-permute-start(f32[8,1,128]{2,1,0:T(1,128)S(1)} %get-tuple-element.80), channel_id=1, source_target_pairs={{1,0},{2,1},{3,2},{4,3},{5,4},{6,5},{7,6},{8,7},{9,8},{10,9},{11,1... | collective-permute-start | bytes 12296 | tf_op jit(solution)/shard_map/ppermute | solution.py:20
  (151 shorter events, 54.1 us)
Async XLA Ops:
  2.1 24.2 %copy-start.23 = (s32[1,1,64]{2,1,0:T(1,128)S(1)}, s32[1,1,64]{2,1,0:T(1,128)}, u32[]{:S(2)}) copy-start(s32[1,1,64]{2,1,0:T(1,128)} %param.12) | copy-start | bytes 772
  2.4 27.6 %collective-permute-start = (bf16[24,8,1,128]{3,2,1,0:T(2,128)(2,1)S(1)}, bf16[24,8,1,128]{3,2,1,0:T(2,128)(2,1)S(1)}, u32[]{:S(2)}, u32[]{:S(2)}) collective-permute-start(bf16[24,8,1,128]{3,2,1,0:T(2,128)(2,1)S(1)} %get-tuple-element.76), channel_id=1, source_target_pairs={{0,1},{1,2},{2,3},{3,4},{4,5},{5,6},{6,7},{7,8},{8,9},{9,10},{10,1... | collective-permute-start | bytes 147464 | tf_op jit(solution)/shard_map/ppermute | solution.py:19
  6.9 23.1 %collective-permute-start.1 = (bf16[24,1,16,128]{3,2,1,0:T(8,128)(2,1)S(1)}, bf16[24,1,16,128]{3,2,1,0:T(8,128)(2,1)S(1)}, u32[]{:S(2)}, u32[]{:S(2)}) collective-permute-start(bf16[24,1,16,128]{3,2,1,0:T(8,128)(2,1)S(1)} %get-tuple-element.74), channel_id=1, source_target_pairs={{0,16},{16,32},{32,48},{48,64},{64,80},{80,96},{96,112},{112,128},... | collective-permute-start | bytes 294920 | tf_op jit(solution)/shard_map/ppermute | solution.py:19
  11.1 18.9 %collective-permute-start.2 = (bf16[24,1,16,128]{3,2,1,0:T(8,128)(2,1)S(1)}, bf16[24,1,16,128]{3,2,1,0:T(8,128)(2,1)S(1)}, u32[]{:S(2)}, u32[]{:S(2)}) collective-permute-start(bf16[24,1,16,128]{3,2,1,0:T(8,128)(2,1)S(1)} %get-tuple-element.75), channel_id=1, source_target_pairs={{16,0},{32,16},{48,32},{64,48},{80,64},{96,80},{112,96},{128,112},... | collective-permute-start | bytes 294920 | tf_op jit(solution)/shard_map/ppermute | solution.py:20
  23.2 6.8 %collective-permute-start.3 = (bf16[24,8,1,128]{3,2,1,0:T(2,128)(2,1)S(1)}, bf16[24,8,1,128]{3,2,1,0:T(2,128)(2,1)S(1)}, u32[]{:S(2)}, u32[]{:S(2)}) collective-permute-start(bf16[24,8,1,128]{3,2,1,0:T(2,128)(2,1)S(1)} %get-tuple-element.77), channel_id=1, source_target_pairs={{1,0},{2,1},{3,2},{4,3},{5,4},{6,5},{7,6},{8,7},{9,8},{10,9},{11,1... | collective-permute-start | bytes 147464 | tf_op jit(solution)/shard_map/ppermute | solution.py:20
  43.9 24.4 %all-to-all-start = ((f32[32,1,512]{2,1,0:T(1,128)}), f32[32,1,512]{2,1,0:T(1,128)S(1)}, u32[]{:S(2)}, u32[]{:S(2)}) async-start(f32[32,1,512]{2,1,0:T(1,128)} %reshape.280), calls=%async_computation | async-start | bytes 131072 | tf_op jit(solution)/shard_map/all_to_all | solution.py:143
  50.7 30.6 %collective-permute-start.4 = (f32[20,1,16,128]{3,2,1,0:T(8,128)}, f32[20,1,16,128]{3,2,1,0:T(8,128)}, u32[]{:S(2)}, u32[]{:S(2)}) collective-permute-start(f32[20,1,16,128]{3,2,1,0:T(8,128)} %get-tuple-element.72), channel_id=1, source_target_pairs={{16,0},{32,16},{48,32},{64,48},{80,64},{96,80},{112,96},{128,112},... | collective-permute-start | bytes 491528 | tf_op jit(solution)/shard_map/ppermute | solution.py:20
  58.2 23.2 %collective-permute-start.5 = (f32[20,1,16,128]{3,2,1,0:T(8,128)}, f32[20,1,16,128]{3,2,1,0:T(8,128)}, u32[]{:S(2)}, u32[]{:S(2)}) collective-permute-start(f32[20,1,16,128]{3,2,1,0:T(8,128)} %get-tuple-element.73), channel_id=1, source_target_pairs={{0,16},{16,32},{32,48},{48,64},{64,80},{80,96},{96,112},{112,128},... | collective-permute-start | bytes 491528 | tf_op jit(solution)/shard_map/ppermute | solution.py:19
  60.9 20.4 %collective-permute-start.6 = (f32[20,8,1,128]{3,2,1,0:T(1,128)}, f32[20,8,1,128]{3,2,1,0:T(1,128)}, u32[]{:S(2)}, u32[]{:S(2)}) collective-permute-start(f32[20,8,1,128]{3,2,1,0:T(1,128)} %get-tuple-element.66), channel_id=1, source_target_pairs={{1,0},{2,1},{3,2},{4,3},{5,4},{6,5},{7,6},{8,7},{9,8},{10,9},{11,1... | collective-permute-start | bytes 245768 | tf_op jit(solution)/shard_map/ppermute | solution.py:20
  66.4 15.0 %collective-permute-start.7 = (f32[20,8,1,128]{3,2,1,0:T(1,128)}, f32[20,8,1,128]{3,2,1,0:T(1,128)}, u32[]{:S(2)}, u32[]{:S(2)}) collective-permute-start(f32[20,8,1,128]{3,2,1,0:T(1,128)} %get-tuple-element.67), channel_id=1, source_target_pairs={{0,1},{1,2},{2,3},{3,4},{4,5},{5,6},{6,7},{7,8},{8,9},{9,10},{10,1... | collective-permute-start | bytes 245768 | tf_op jit(solution)/shard_map/ppermute | solution.py:19
  69.5 11.9 %copy-start.5 = (f32[8,16,128]{2,1,0:T(8,128)S(1)}, f32[8,16,128]{2,1,0:T(8,128)}, u32[]{:S(2)}) copy-start(f32[8,16,128]{2,1,0:T(8,128)} %copy-done.4) | copy-start | bytes 196612
  69.5 11.9 %copy-start.7 = (f32[8,16,128]{2,1,0:T(8,128)S(1)}, f32[8,16,128]{2,1,0:T(8,128)}, u32[]{:S(2)}) copy-start(f32[8,16,128]{2,1,0:T(8,128)} %copy-done.6) | copy-start | bytes 196612
  69.5 11.9 %copy-start.9 = (f32[8,16,128]{2,1,0:T(8,128)S(1)}, f32[8,16,128]{2,1,0:T(8,128)}, u32[]{:S(2)}) copy-start(f32[8,16,128]{2,1,0:T(8,128)} %copy-done.8) | copy-start | bytes 196612
  69.6 11.9 %copy-start.11 = (f32[8,16,128]{2,1,0:T(8,128)S(1)}, f32[8,16,128]{2,1,0:T(8,128)}, u32[]{:S(2)}) copy-start(f32[8,16,128]{2,1,0:T(8,128)} %copy-done.10) | copy-start | bytes 196612
  75.8 11.3 %all-to-all-start.1 = ((bf16[16,2,512]{2,1,0:T(2,128)(2,1)}), bf16[16,2,512]{2,1,0:T(2,128)(2,1)S(1)}, u32[]{:S(2)}, u32[]{:S(2)}) async-start(bf16[16,2,512]{2,1,0:T(2,128)(2,1)} %reshape.282), calls=%async_computation.1 | async-start | bytes 65536 | tf_op jit(solution)/shard_map/all_to_all | solution.py:145
  91.9 11.5 %all-to-all-start.2 = ((f32[16,1,1024]{2,1,0:T(1,128)}), f32[16,1,1024]{2,1,0:T(1,128)S(1)}, u32[]{:S(2)}, u32[]{:S(2)}) async-start(f32[16,1,1024]{2,1,0:T(1,128)} %reshape.284), calls=%async_computation.2 | async-start | bytes 131072 | tf_op jit(solution)/shard_map/all_to_all | solution.py:158
  105.1 11.7 %copy-start.3 = (bf16[20,400]{1,0:T(8,128)(2,1)S(1)}, bf16[20,400]{1,0:T(8,128)(2,1)}, u32[]{:S(2)}) copy-start(bf16[20,400]{1,0:T(8,128)(2,1)} %param.15) | copy-start | bytes 48004
  105.1 11.7 %copy-start.22 = (bf16[800,20]{0,1:T(8,128)(2,1)S(1)}, bf16[800,20]{0,1:T(8,128)(2,1)}, u32[]{:S(2)}) copy-start(bf16[800,20]{0,1:T(8,128)(2,1)} %param.13) | copy-start | bytes 96004
  107.8 41.2 %all-to-all-start.3 = ((f32[32,1,512]{2,1,0:T(1,128)}), f32[32,1,512]{2,1,0:T(1,128)S(1)}, u32[]{:S(2)}, u32[]{:S(2)}) async-start(f32[32,1,512]{2,1,0:T(1,128)} %reshape.286), calls=%async_computation.3 | async-start | bytes 131072 | tf_op jit(solution)/shard_map/all_to_all | solution.py:160
  116.8 27.7 %copy-start.20 = (s32[64]{0:T(128)S(1)}, s32[64]{0:T(128)}, u32[]{:S(2)}) copy-start(s32[64]{0:T(128)} %get-tuple-element.97) | copy-start | bytes 772
  151.7 15.5 %collective-permute-start.8 = (f32[1,16,128]{2,1,0:T(8,128)S(1)}, f32[1,16,128]{2,1,0:T(8,128)S(1)}, u32[]{:S(2)}, u32[]{:S(2)}) collective-permute-start(f32[1,16,128]{2,1,0:T(8,128)S(1)} %get-tuple-element.83), channel_id=1, source_target_pairs={{16,0},{32,16},{48,32},{64,48},{80,64},{96,80},{112,96},{128,112},... | collective-permute-start | bytes 24584 | tf_op jit(solution)/shard_map/ppermute | solution.py:20
  158.9 8.6 %collective-permute-start.9 = (f32[1,16,128]{2,1,0:T(8,128)S(1)}, f32[1,16,128]{2,1,0:T(8,128)S(1)}, u32[]{:S(2)}, u32[]{:S(2)}) collective-permute-start(f32[1,16,128]{2,1,0:T(8,128)S(1)} %get-tuple-element.82), channel_id=1, source_target_pairs={{0,16},{16,32},{32,48},{48,64},{64,80},{80,96},{96,112},{112,128},... | collective-permute-start | bytes 24584 | tf_op jit(solution)/shard_map/ppermute | solution.py:19
  160.8 5.7 %collective-permute-start.10 = (f32[8,1,128]{2,1,0:T(1,128)S(1)}, f32[8,1,128]{2,1,0:T(1,128)S(1)}, u32[]{:S(2)}, u32[]{:S(2)}) collective-permute-start(f32[8,1,128]{2,1,0:T(1,128)S(1)} %get-tuple-element.80), channel_id=1, source_target_pairs={{1,0},{2,1},{3,2},{4,3},{5,4},{6,5},{7,6},{8,7},{9,8},{10,9},{11,1... | collective-permute-start | bytes 12296 | tf_op jit(solution)/shard_map/ppermute | solution.py:20
  164.1 3.1 %collective-permute-start.11 = (f32[8,1,128]{2,1,0:T(1,128)S(1)}, f32[8,1,128]{2,1,0:T(1,128)S(1)}, u32[]{:S(2)}, u32[]{:S(2)}) collective-permute-start(f32[8,1,128]{2,1,0:T(1,128)S(1)} %get-tuple-element.81), channel_id=1, source_target_pairs={{0,1},{1,2},{2,3},{3,4},{4,5},{5,6},{6,7},{7,8},{8,9},{9,10},{10,1... | collective-permute-start | bytes 12296 | tf_op jit(solution)/shard_map/ppermute | solution.py:19
  (18 other events, 43.1 us)
where the time goes:
time: 172 us; the launch traced here: 168 us
  starting transfers between devices  81.2 us (47%)
  matrix products  37.5 us (22%)
  other arithmetic  21.5 us (12%)
  local copies, waits for them, and re-layouts  20.6 us (12%)
  waiting for transfers between devices  5.93 us (3%)
    ppermute x6, starting transfers between devices, padded_2(): lax.ppermute(initial, axis, [(b, a) for a, b in up])  37.4 us
    dot_general x8, matrix products, evaluate(): jnp.einsum('kh,bhz->bkz', w_mid, hidden_one, preferred_element_type=jnp.f...  25.9 us
    ppermute x6, starting transfers between devices, padded_2(): lax.ppermute(last, axis, up)  16.8 us
    all_to_all x1, starting transfers between devices, shards(): lax.all_to_all(solved, 'gx', split_axis=0, concat_axis=2, tiled=True)  8.97 us
    unnamed x61, local copies, waits for them, and re-layouts  8.14 us
    all_to_all x1, starting transfers between devices, shards(): lax.all_to_all(spectrum, 'gx', split_axis=2, concat_axis=0, tiled=True)  6.8 us
    all_to_all x1, starting transfers between devices, shards(): lax.all_to_all(solved, 'gy', split_axis=1, concat_axis=0, tiled=True)  5.72 us
    all_to_all x1, starting transfers between devices, shards(): lax.all_to_all(along_x.astype(jnp.bfloat16), 'gy', split_axis=0, concat_a...  5.52 us
  transfers between devices with their start and end apart: 16, of which 3 were waited for; matrix products, arithmetic and copies ran while one was open for 31% of the time, Pallas kernels for 0%

commit v1 on v0

v1 whole, which is shorter than its diff:
```python
import math

import jax
import jax.numpy as jnp
import numpy as np
from jax import lax
from jax.experimental import pallas as pl
from jax.experimental.pallas import tpu as pltpu
from jax.sharding import PartitionSpec as P

time_step = 0.25
f32 = jnp.float32
bf16 = jnp.bfloat16


def split_table(table):
    high = np.asarray(table, np.float64).astype(jnp.bfloat16)
    low = (np.asarray(table, np.float64) - high.astype(np.float64)).astype(jnp.bfloat16)
    return high, low


def product(left, right, contract):
    return lax.dot_general(left, right, (contract, ((), ())), preferred_element_type=f32)


def halves(value):
    high = value.astype(bf16)
    return high, (value - high.astype(f32)).astype(bf16)


def right_table(value, table_high, table_low):
    contract = ((1,), (0,))
    high, low = halves(value)
    return (
        product(high, table_high, contract)
        + product(low, table_high, contract)
        + product(high, table_low, contract)
    )


def times(pair, factor):
    real, imag = pair
    c, s = float(np.real(factor)), float(np.imag(factor))
    if abs(s) < 1e-12:
        return (real, imag) if c > 0 else (-real, -imag)
    if abs(c) < 1e-12:
        return (-imag, real) if s > 0 else (imag, -real)
    if abs(abs(c) - abs(s)) < 1e-12:
        size = abs(c)
        sc, ss = (1 if c > 0 else -1), (1 if s > 0 else -1)
        first = real * size
        second = imag * size
        new_real = (first if sc > 0 else -first) - (second if ss > 0 else -second)
        new_imag = (first if ss > 0 else -first) + (second if sc > 0 else -second)
        return new_real, new_imag
    return real * c - imag * s, real * s + imag * c


def complex_dft(values):
    count = len(values)
    if count == 1:
        return values
    even = complex_dft(values[0::2])
    odd = complex_dft(values[1::2])
    half = count // 2
    low, high = [], []
    for k in range(half):
        turned = times(odd[k], np.exp(-2j * np.pi * k / count))
        low.append((even[k][0] + turned[0], even[k][1] + turned[1]))
        high.append((even[k][0] - turned[0], even[k][1] - turned[1]))
    return low + high


def real_dft(values):
    count = len(values)
    if count == 2:
        zero = jnp.zeros_like(values[0])
        return [(values[0] + values[1], zero), (values[0] - values[1], zero)]
    even = real_dft(values[0::2])
    odd = real_dft(values[1::2])
    half = count // 2
    out = [None] * (half + 1)
    for k in range(half // 2 + 1):
        turned = times(odd[k], np.exp(-2j * np.pi * k / count))
        out[half - k] = (even[k][0] - turned[0], turned[1] - even[k][1])
        out[k] = (even[k][0] + turned[0], even[k][1] + turned[1])
    return out


def full_spectrum(values):
    half = real_dft(values)
    count = len(values)
    return [half[k] if k <= count // 2 else (half[count - k][0], -half[count - k][1]) for k in range(count)]


def turn(pair, cosine, sine):
    real, imag = pair
    return real * cosine + imag * sine, imag * cosine - real * sine


def lane_index(shape):
    return lax.broadcasted_iota(jnp.int32, shape, len(shape) - 1)


def central(values, step, roll):
    count = len(values)
    lane = lane_index(values[0].shape)
    if step == 16:
        digit, top, back = lane // 16, 7, -16
        forward_from_other, backward_from_other = -16, 16
    else:
        digit, top = lane % 16, 15
        forward_from_other, backward_from_other = 15, -15
    last, first = digit == top, digit == 0
    up = [roll(v, -step) for v in values]
    down = [roll(v, step) for v in values]
    up_other = up if step == 16 else [roll(v, forward_from_other) for v in values]
    down_other = down if step == 16 else [roll(v, backward_from_other) for v in values]
    out = []
    for n in range(count):
        after = jnp.where(last, up_other[(n + 1) % count], up[n])
        before = jnp.where(first, down_other[(n - 1) % count], down[n])
        out.append(0.5 * (after - before))
    return out


def depth_modes(velocity, tables):
    plain, derived = tables
    fields = []
    for n in range(3):
        table_high, table_low = plain if n < 2 else derived
        high, low = halves(velocity[n])
        contract = ((1,), (1,))
        fields.append(
            product(table_high, high, contract)
            + product(table_high, low, contract)
            + product(table_low, high, contract)
        )
    return [
        jnp.concatenate([f[4 * n : 4 * n + 4] for f in fields], 0) for n in range(32)
    ]


def forward_x(values, turn_cos, turn_sin, table, roll):
    slope = central([v[0:8] for v in values], 16, roll)
    lines = [
        jnp.concatenate([s[0:4] + v[8:12], v[4:8]], 0) for s, v in zip(slope, values)
    ]
    modes = full_spectrum(lines)
    rows = []
    for k, pair in enumerate(modes):
        rows.append(jnp.concatenate(turn(pair, turn_cos[k : k + 1], turn_sin[k : k + 1]), 1))
    return right_table(jnp.concatenate(rows, 0), *table)


def middle_y(values, turn_cos, turn_sin, table, table_back, eigen_xz, eigen_y, roll):
    plain = [jnp.concatenate([v[0:4], v[8:12]], 0) for v in values]
    other = [jnp.concatenate([v[4:8], v[12:16]], 0) for v in values]
    lines = [p + s for p, s in zip(plain, central(other, 1, roll))]
    rows = []
    for k, pair in enumerate(full_spectrum(lines)):
        rows.append(jnp.concatenate(turn(pair, turn_cos[k : k + 1], turn_sin[k : k + 1]), 1))
    modes = right_table(jnp.concatenate(rows, 0), *table)
    scaled = []
    for k in range(16):
        eigen = eigen_xz + eigen_y[k : k + 1]
        mean_mode = eigen == 0.0
        scale = jnp.where(mean_mode, 0.0, (-1.0 / 65536.0) / jnp.where(mean_mode, 1.0, eigen))
        scaled.append(modes[8 * k : 8 * k + 8] * scale)
    back = right_table(jnp.concatenate(scaled, 0), *table_back)
    pairs = []
    for k in range(16):
        row = back[8 * k : 8 * k + 8]
        pairs.append(turn((row[:, :128], row[:, 128:]), turn_cos[k : k + 1], turn_sin[k : k + 1]))
    pressure = [real - imag for real, imag in complex_dft(pairs)]
    slope = central(pressure, 1, roll)
    return [
        jnp.concatenate([p[0:4], s[0:4], p[4:8], s[4:8]], 0) for p, s in zip(pressure, slope)
    ]


def backward_x(modes, turn_cos, turn_sin, table_back, roll):
    back = right_table(modes, *table_back)
    pairs = []
    for k in range(32):
        row = back[8 * k : 8 * k + 8]
        pairs.append(turn((row[:, :128], row[:, 128:]), turn_cos[k : k + 1], turn_sin[k : k + 1]))
    lines = [real - imag for real, imag in complex_dft(pairs)]
    slope = central(lines, 16, roll)
    return [
        jnp.concatenate([s[0:4], v[4:8], v[0:4]], 0) for s, v in zip(slope, lines)
    ]


def depth_back(fields, velocity, tables):
    plain, derived = tables
    out = []
    for n in range(3):
        table_high, table_low = plain if n < 2 else derived
        turned = fields[n].T.astype(bf16)
        contract = ((1,), (0,))
        gradient = product(turned, table_high, contract) + product(turned, table_low, contract)
        out.append(velocity[n] - gradient)
    return out


def cosine_numpy(length):
    position = np.arange(length)
    weight = np.where(position == 0, math.sqrt(1.0 / length), math.sqrt(2.0 / length))
    return weight[:, None] * np.cos(np.pi / (2 * length) * position[:, None] * (2 * position[None, :] + 1))


def make_tables():
    t = {}
    cosine = cosine_numpy(128)
    above = np.concatenate([cosine[:, 1:], cosine[:, -1:]], 1)
    below = np.concatenate([cosine[:, :1], cosine[:, :-1]], 1)
    t["depth"] = split_table(cosine)
    t["depth_back_slope"] = split_table(0.5 * (above - below))
    slope = np.zeros((128, 128))
    for z in range(128):
        slope[z, min(z + 1, 127)] += 0.5
        slope[z, max(z - 1, 0)] -= 0.5
    t["depth_slope"] = split_table(cosine @ slope)

    def digits(points):
        angle = 2 * np.pi / points * np.outer(np.arange(points), np.arange(points))
        return angle

    eight, sixteen = digits(8), digits(16)
    one16, one8 = np.eye(16), np.eye(8)
    t["x"] = split_table(
        np.concatenate(
            [np.kron(np.cos(eight) + np.sin(eight), one16), np.kron(np.sin(eight) - np.cos(eight), one16)], 0
        )
    )
    t["y"] = split_table(
        np.concatenate(
            [np.kron(one8, np.cos(sixteen) + np.sin(sixteen)), np.kron(one8, np.sin(sixteen) - np.cos(sixteen))], 0
        )
    )
    t["x_back"] = split_table(
        np.concatenate([np.kron(np.cos(eight), one16), np.kron(-np.sin(eight), one16)], 1)
    )
    t["y_back"] = split_table(
        np.concatenate([np.kron(one8, np.cos(sixteen)), np.kron(one8, -np.sin(sixteen))], 1)
    )
    lane = np.arange(128)
    turn_x = 2 * np.pi / 256 * np.outer(np.arange(32), lane // 16)
    turn_y = 2 * np.pi / 256 * np.outer(np.arange(16), lane % 16)
    t["turn_x"] = (np.cos(turn_x).astype(np.float32), np.sin(turn_x).astype(np.float32))
    t["turn_y"] = (np.cos(turn_y).astype(np.float32), np.sin(turn_y).astype(np.float32))
    k1 = np.arange(32)
    eigen_x = 2 - 2 * np.cos(2 * np.pi / 256 * (k1[:, None] + 32 * (lane // 16)[None, :]))
    t["eigen_x"] = np.repeat(eigen_x.reshape(16, 2, 128), 4, axis=1).astype(np.float32)
    kz = 2 - 2 * np.cos(np.pi * np.arange(128) / 128)
    t["eigen_z"] = np.ascontiguousarray(
        np.broadcast_to(np.tile(kz.reshape(32, 4), (1, 2))[:, :, None], (32, 8, 128))
    ).astype(np.float32)
    t["eigen_y"] = (
        2 - 2 * np.cos(2 * np.pi / 256 * (np.arange(16)[:, None] + 16 * (lane % 16)[None, :]))
    ).astype(np.float32)
    return t


def whole(shape):
    return pl.BlockSpec(shape, lambda *_: (0,) * len(shape))


def lane_roll(value, shift):
    return pltpu.roll(value, shift % 128, 1)


def call(body, out_shape, operands, name, limit=16):
    return pl.pallas_call(
        body,
        out_shape=out_shape,
        compiler_params=pltpu.CompilerParams(vmem_limit_bytes=limit << 20),
        name=name,
    )(*operands)


def depth_kernel(velocity, th, tl, sh, sl, out):
    values = [velocity[n] for n in range(3)]
    groups = depth_modes(values, ((th[...], tl[...]), (sh[...], sl[...])))
    for n, group in enumerate(groups):
        out[n] = group.astype(bf16)


def forward_kernel(values, tc, ts, th, tl, out):
    modes = forward_x(
        [values[n].astype(f32) for n in range(32)], tc[...], ts[...], (th[...], tl[...]), lane_roll
    )
    out[...] = modes.reshape(16, 16, 128)


def middle_kernel(place, values, tc, ts, th, tl, bh, bl, ex, ez, ey, out):
    result = middle_y(
        [values[n] for n in range(16)],
        tc[...],
        ts[...],
        (th[...], tl[...]),
        (bh[...], bl[...]),
        ex[place[1]] + ez[place[0]],
        ey[...],
        lane_roll,
    )
    for n, value in enumerate(result):
        out[n] = value


def backward_kernel(values, tc, ts, bh, bl, out):
    result = backward_x(values[...].reshape(256, 128), tc[...], ts[...], (bh[...], bl[...]), lane_roll)
    for n, value in enumerate(result):
        out[n] = value.astype(bf16)


def last_kernel(values, velocity, th, tl, sh, sl, out):
    loaded = [values[n].astype(f32) for n in range(32)]
    fields = [jnp.concatenate([v[4 * n : 4 * n + 4] for v in loaded], 0) for n in range(3)]
    result = depth_back(
        fields, [velocity[n] for n in range(3)], ((th[...], tl[...]), (sh[...], sl[...]))
    )
    for n, value in enumerate(result):
        out[n] = value


def project(velocity):
    t = make_tables()
    columns = velocity.reshape(3, 128, 128)
    modes = call(
        depth_kernel,
        jax.ShapeDtypeStruct((32, 12, 128), bf16),
        (columns, *t["depth"], *t["depth_slope"]),
        "depth_modes",
    )
    modes = lax.all_to_all(modes, "gx", split_axis=0, concat_axis=0, tiled=True)
    modes = call(
        forward_kernel,
        jax.ShapeDtypeStruct((16, 16, 128), f32),
        (modes, *t["turn_x"], *t["x"]),
        "forward_x",
    )
    modes = lax.all_to_all(modes, "gy", split_axis=0, concat_axis=0, tiled=True)
    place = jnp.stack([lax.axis_index("gx"), lax.axis_index("gy")]).astype(jnp.int32)
    modes = pl.pallas_call(
        middle_kernel,
        out_shape=jax.ShapeDtypeStruct((16, 16, 128), f32),
        in_specs=[pl.BlockSpec(memory_space=pltpu.SMEM)] + [pl.BlockSpec(memory_space=pltpu.VMEM)] * 10,
        compiler_params=pltpu.CompilerParams(vmem_limit_bytes=16 << 20),
        name="middle_y",
    )(place, modes, *t["turn_y"], *t["y"], *t["y_back"], t["eigen_x"], t["eigen_z"], t["eigen_y"])
    modes = lax.all_to_all(modes, "gy", split_axis=0, concat_axis=0, tiled=True)
    modes = call(
        backward_kernel,
        jax.ShapeDtypeStruct((32, 12, 128), bf16),
        (modes, *t["turn_x"], *t["x_back"]),
        "backward_x",
    )
    modes = lax.all_to_all(modes, "gx", split_axis=0, concat_axis=0, tiled=True)
    result = call(
        last_kernel,
        jax.ShapeDtypeStruct((3, 128, 128), f32),
        (modes, columns, *t["depth"], *t["depth_back_slope"]),
        "depth_back",
    )
    return result.reshape(velocity.shape)


def padded_2(value, sides, width):
    edges = {}
    for axis, dim in sides:
        size, length = (lax.axis_size(axis), value.shape[dim])
        up = [(i, (i + 1) % size) for i in range(size)]
        last = lax.slice_in_dim(value, length - width, length, axis=dim)
        initial = lax.slice_in_dim(value, 0, width, axis=dim)
        edges[dim] = (
            lax.ppermute(last.astype(bf16), axis, up).astype(value.dtype),
            lax.ppermute(initial.astype(bf16), axis, [(b, a) for a, b in up]).astype(value.dtype),
        )
    done = []
    for _, dim in sides:
        low, high = edges[dim]
        around = [(width, width) if d in done else (0, 0) for d in range(value.ndim)]
        value = jnp.concatenate([jnp.pad(low, around), value, jnp.pad(high, around)], axis=dim)
        done.append(dim)
    return value


def depth_next(values):
    return jnp.concatenate([values[..., 1:], values[..., -1:]], -1)


def depth_prev(values):
    return jnp.concatenate([values[..., :1], values[..., :-1]], -1)


def transport_rate(field_pad, flow_pad):
    center = field_pad[:, 1:-1, 1:-1]
    x_next = field_pad[:, 2:, 1:-1]
    x_prev = field_pad[:, :-2, 1:-1]
    y_next = field_pad[:, 1:-1, 2:]
    y_prev = field_pad[:, 1:-1, :-2]
    z_next = depth_next(center)
    z_prev = depth_prev(center)
    coefficient = flow_pad[3, 1:-1, 1:-1]
    advection = (
        flow_pad[0, 1:-1, 1:-1] * (x_next - x_prev) * 0.5
        + flow_pad[1, 1:-1, 1:-1] * (y_next - y_prev) * 0.5
        + flow_pad[2, 1:-1, 1:-1] * (z_next - z_prev) * 0.5
    )
    diffusion = 0.5 * (coefficient + flow_pad[3, 2:, 1:-1]) * (x_next - center) - 0.5 * (
        coefficient + flow_pad[3, :-2, 1:-1]
    ) * (center - x_prev)
    diffusion = (
        diffusion
        + 0.5 * (coefficient + flow_pad[3, 1:-1, 2:]) * (y_next - center)
        - 0.5 * (coefficient + flow_pad[3, 1:-1, :-2]) * (center - y_prev)
    )
    diffusion = (
        diffusion
        + 0.5 * (coefficient + depth_next(coefficient)) * (z_next - center)
        - 0.5 * (coefficient + depth_prev(coefficient)) * (center - z_prev)
    )
    return diffusion - advection


def network(blocks, w_in, w_mid, w_out):
    block_count = blocks.shape[0]
    bundle_size = 8
    padded_count = -(-block_count // bundle_size) * bundle_size

    def evaluate(bundle):
        hidden_one = jnp.einsum("hn,bnz->bhz", w_in, bundle, preferred_element_type=jnp.float32)
        hidden_one = jax.nn.gelu(hidden_one).astype(jnp.bfloat16)
        hidden_two = jnp.einsum(
            "kh,bhz->bkz", w_mid, hidden_one, preferred_element_type=jnp.float32
        )
        hidden_two = jax.nn.gelu(hidden_two).astype(jnp.bfloat16)
        return jnp.einsum("nk,bkz->bnz", w_out, hidden_two, preferred_element_type=jnp.float32)

    reaction = lax.map(
        evaluate, blocks.reshape((padded_count // bundle_size, bundle_size) + blocks.shape[1:])
    )
    return reaction.reshape((padded_count,) + reaction.shape[2:])


def shards(scalars, velocity, diffusivity, burn_list, w_in, w_mid, w_out):
    channels = scalars.shape[0]
    joined = jnp.concatenate([scalars, diffusivity[None]], 0)
    padded = padded_2(joined, (("gx", 1), ("gy", 2)), 1)
    field_pad = padded[:channels]
    around = ((0, 0), (1, 1), (1, 1), (0, 0))
    inner_flow = jnp.concatenate([jnp.pad(velocity, around), padded[channels:]], 0)
    section_one = scalars + time_step * transport_rate(field_pad, inner_flow)
    section_pad = padded_2(section_one, (("gx", 1), ("gy", 2)), 1)
    transported = 0.5 * scalars + 0.5 * (
        section_one + time_step * transport_rate(section_pad, inner_flow)
    )
    velocity_out = project(velocity)
    cells_x, cells_y, depth = scalars.shape[1:]
    block_total = cells_x * cells_y
    flat_blocks = transported.reshape(channels, block_total, depth)
    listed = burn_list.reshape(-1)
    picked = jnp.take(flat_blocks, jnp.minimum(listed, block_total - 1), axis=1)
    chosen = jnp.transpose(picked, (1, 0, 2)).astype(jnp.bfloat16)
    own_rates = network(chosen, w_in, w_mid, w_out)
    updated = flat_blocks.at[:, listed].add(jnp.transpose(own_rates, (1, 0, 2)), mode="drop")
    scalars_out = updated.reshape(transported.shape)
    return (scalars_out, velocity_out)


def solution(mesh):
    in_specs = (
        P(None, "gx", "gy", None),
        P(None, "gx", "gy", None),
        P("gx", "gy", None),
        P("gx", "gy", None),
        P(),
        P(),
        P(),
    )
    out_specs = (P(None, "gx", "gy", None), P(None, "gx", "gy", None))
    return jax.shard_map(shards, mesh=mesh, in_specs=in_specs, out_specs=out_specs, check_vma=False)
```

time: 172 us -> 153 us (0.89); the launches traced: 168 us -> 152 us
  starting transfers between devices: 81.2 us -> 66.6 us
  local copies, waits for them, and re-layouts: 20.6 us -> 13 us
  Pallas kernels: 0 us -> 6.01 us
  other arithmetic: 21.5 us -> 27.2 us
  matrix products: 37.5 us -> 32.8 us
    ppermute x12 -> x8, starting transfers between devices: 54.2 us -> 39 us  [the longest x4 27.1 us: padded_2(): lax.ppermute(initial.astype(bf16), axis, [(b, a) for a, b in up])]
    dot_general x6 -> x0, matrix products: 9.87 us -> none  [the longest x1 3.41 us: shards(): along_x = jnp.einsum('cx,xyz->cyz', table_x, along_x, precision=highest)]
    unnamed x61 -> x83, local copies, waits for them, and re-layouts: 8.14 us -> 1.5 us
    pallas_call x0 -> x5, Pallas kernels: none -> 6.01 us  [the longest x4 4.08 us: call(): pl.pallas_call(body, out_shape=out_shape, compiler_params=pltpu.CompilerP...]
    dot_general x8, matrix products: 1.71 us -> 6.95 us  [evaluate(): jnp.einsum('nk,bkz->bnz', w_out, hidden_two, preferred_element_type=jnp.f...]
    all_to_all x4, waiting for transfers between devices: 4.92 us -> 0.01 us  [the longest x2 0.01 us: project(): modes = lax.all_to_all(modes, 'gx', split_axis=0, concat_axis=0, tiled=True)]
    pad x0 -> x4, other arithmetic: none -> 4.35 us  [the longest x2 2.61 us: padded_2(): jnp.pad(low, around)]
    ppermute x12 -> x8, waiting for transfers between devices: 1.01 us -> 4.52 us  [the longest x4 2.3 us: padded_2(): lax.ppermute(last.astype(bf16), axis, up).astype(value.dtype)]
  transfers between devices with their start and end apart: 16 -> 12, of which waited for: 3 -> 2; matrix products, arithmetic and copies ran while one was open for 31% -> 47% of each run, Pallas kernels for 0% -> 1%
where the time goes in v1:
time: 153 us; the launch traced here: 152 us
  starting transfers between devices  66.6 us (44%)
  matrix products  32.8 us (21%)
  other arithmetic  27.2 us (18%)
  local copies, waits for them, and re-layouts  13 us (8%)
  Pallas kernels  6.01 us (4%)
  waiting for transfers between devices  4.54 us (3%)
    ppermute x4, starting transfers between devices, padded_2(): lax.ppermute(initial.astype(bf16), axis, [(b, a) for a, b in up])  27.1 us
    dot_general x8, matrix products, evaluate(): jnp.einsum('kh,bhz->bkz', w_mid, hidden_one, preferred_element_type=jnp.f...  25.8 us
    all_to_all x2, starting transfers between devices, project(): modes = lax.all_to_all(modes, 'gx', split_axis=0, concat_axis=0, tiled=True)  15.1 us
    all_to_all x2, starting transfers between devices, project(): modes = lax.all_to_all(modes, 'gy', split_axis=0, concat_axis=0, tiled=True)  12.5 us
    ppermute x4, starting transfers between devices, padded_2(): lax.ppermute(last.astype(bf16), axis, up).astype(value.dtype)  11.8 us
    slice x6, local copies, waits for them, and re-layouts, depth_next(): return jnp.concatenate([values[..., 1:], values[..., -1:]], -1)  8.35 us
    dot_general x8, matrix products, evaluate(): jnp.einsum('nk,bkz->bnz', w_out, hidden_two, preferred_element_type=jnp.f...  6.95 us
    scatter-add x1, other arithmetic, shards(): flat_blocks.at[:, listed]  5.96 us
  transfers between devices with their start and end apart: 12, of which 2 were waited for; matrix products, arithmetic and copies ran while one was open for 47% of the time, Pallas kernels for 1%

profile of v1, /device:TPU:1, one launch (start us, length us, event | category | flops | bytes accessed | tf_op | source)
XLA Modules:
  0.0 151.6 jit_solution(2492606391480706481)
XLA Ops:
  2.5 15.2 %collective-permute-start = (bf16[21,1,16,128]{3,2,1,0:T(8,128)(2,1)}, bf16[21,1,16,128]{3,2,1,0:T(8,128)(2,1)}, u32[]{:S(2)}, u32[]{:S(2)}) collective-permute-start(bf16[21,1,16,128]{3,2,1,0:T(8,128)(2,1)} %get-tuple-element.58), channel_id=1, source_target_pairs={{16,0},{32,16},{48,32},{64,48},{80,64},{96,80},{112,96},{128,112},... | collective-permute-start | bytes 258056 | tf_op jit(solution)/shard_map/ppermute | solution.py:379
  20.4 3.9 %collective-permute-start.3 = (bf16[21,8,1,128]{3,2,1,0:T(2,128)(2,1)}, bf16[21,8,1,128]{3,2,1,0:T(2,128)(2,1)}, u32[]{:S(2)}, u32[]{:S(2)}) collective-permute-start(bf16[21,8,1,128]{3,2,1,0:T(2,128)(2,1)} %get-tuple-element.56), channel_id=1, source_target_pairs={{0,1},{1,2},{2,3},{3,4},{4,5},{5,6},{6,7},{7,8},{8,9},{9,10},{10,1... | collective-permute-start | bytes 129032 | tf_op jit(solution)/shard_map/ppermute | solution.py:378
  27.4 7.6 %all-to-all-start = ((bf16[32,12,128]{2,1,0:T(8,128)(2,1)}), bf16[32,12,128]{2,1,0:T(8,128)(2,1)S(1)}, u32[]{:S(2)}, u32[]{:S(2)}) async-start(bf16[32,12,128]{2,1,0:T(8,128)(2,1)} %depth_modes.1), calls=%async_computation | async-start | bytes 262144 | tf_op jit(solution)/shard_map/all_to_all | solution.py:337
  44.6 4.7 %fusion.81 = (bf16[20,8,16,128]{3,2,1,0:T(8,128)(2,1)S(1)}, f32[20,8,16,128]{3,2,1,0:T(8,128)S(1)}) fusion(f32[20,8,16,128]{3,2,1,0:T(8,128)S(1)} %copy-done.22, f32[8,16,128]{2,1,0:T(8,128)S(1)} %get-tuple-element.73, f32[8,16,128]{2,1,0:T(8,128)S(1)} %get-tuple-element.72, f32[8,16,128]{2,1,0:T(8,128)S(1)} %get-tuple-element.71, ...), kind=kLoop, calls=%fused_computation.131 | loop fusion | flops 14417920 | bytes 7112704 | tf_op jit(solution)/shard_map/convert.11
  49.4 2.1 %fusion.83 = (f32[20,8,16,127]{3,2,1,0:T(8,128)}, f32[20,8,16,127]{3,2,1,0:T(8,128)}) fusion(f32[20,8,16,128]{3,2,1,0:T(8,128)S(1)} %get-tuple-element.50), kind=kLoop, calls=%fused_computation.132 | loop fusion | bytes 5201920 | tf_op jit(solution)/shard_map/slice | solution.py:391
  52.4 4.1 %collective-permute-start.7 = (bf16[20,8,1,128]{3,2,1,0:T(2,128)(2,1)}, bf16[20,8,1,128]{3,2,1,0:T(2,128)(2,1)}, u32[]{:S(2)}, u32[]{:S(2)}) collective-permute-start(bf16[20,8,1,128]{3,2,1,0:T(2,128)(2,1)} %get-tuple-element.68), channel_id=1, source_target_pairs={{0,1},{1,2},{2,3},{3,4},{4,5},{5,6},{6,7},{7,8},{8,9},{9,10},{10,1... | collective-permute-start | bytes 122888 | tf_op jit(solution)/shard_map/ppermute | solution.py:378
  59.6 6.3 %all-to-all-start.1 = ((f32[16,16,128]{2,1,0:T(8,128)}), f32[16,16,128]{2,1,0:T(8,128)S(1)}, u32[]{:S(2)}, u32[]{:S(2)}) async-start(f32[16,16,128]{2,1,0:T(8,128)} %forward_x.1), calls=%async_computation.1 | async-start | bytes 262144 | tf_op jit(solution)/shard_map/all_to_all | solution.py:344
  66.8 7.7 %collective-permute-start.4 = (bf16[20,1,16,128]{3,2,1,0:T(8,128)(2,1)S(1)}, bf16[20,1,16,128]{3,2,1,0:T(8,128)(2,1)S(1)}, u32[]{:S(2)}, u32[]{:S(2)}) collective-permute-start(bf16[20,1,16,128]{3,2,1,0:T(8,128)(2,1)S(1)} %get-tuple-element.69), channel_id=1, source_target_pairs={{16,0},{32,16},{48,32},{64,48},{80,64},{96,80},{112,96},{128,112},... | collective-permute-start | bytes 245768 | tf_op jit(solution)/shard_map/ppermute | solution.py:379
  76.5 2.3 %collective-permute-start.6 = (bf16[20,8,1,128]{3,2,1,0:T(2,128)(2,1)}, bf16[20,8,1,128]{3,2,1,0:T(2,128)(2,1)S(1)}, u32[]{:S(2)}, u32[]{:S(2)}) collective-permute-start(bf16[20,8,1,128]{3,2,1,0:T(2,128)(2,1)} %get-tuple-element.67), channel_id=1, source_target_pairs={{1,0},{2,1},{3,2},{4,3},{5,4},{6,5},{7,6},{8,7},{9,8},{10,9},{11,1... | collective-permute-start | bytes 122888 | tf_op jit(solution)/shard_map/ppermute | solution.py:379
  80.4 2.2 %collective-permute-done.6 = bf16[20,8,1,128]{3,2,1,0:T(2,128)(2,1)S(1)} collective-permute-done((bf16[20,8,1,128]{3,2,1,0:T(2,128)(2,1)}, bf16[20,8,1,128]{3,2,1,0:T(2,128)(2,1)S(1)}, u32[]{:S(2)}, u32[]{:S(2)}) %collective-permute-start.6) | collective-permute-done | bytes 40992 | tf_op jit(solution)/shard_map/ppermute | solution.py:379
  84.0 2.3 %collective-permute-done.5 = bf16[20,1,16,128]{3,2,1,0:T(8,128)(2,1)S(1)} collective-permute-done((bf16[20,1,16,128]{3,2,1,0:T(8,128)(2,1)S(1)}, bf16[20,1,16,128]{3,2,1,0:T(8,128)(2,1)S(1)}, u32[]{:S(2)}, u32[]{:S(2)}) %collective-permute-start.5) | collective-permute-done | bytes 81952 | tf_op jit(solution)/shard_map/ppermute | solution.py:378
  89.0 6.2 %all-to-all-start.2 = ((f32[16,16,128]{2,1,0:T(8,128)}), f32[16,16,128]{2,1,0:T(8,128)S(1)}, u32[]{:S(2)}, u32[]{:S(2)}) async-start(f32[16,16,128]{2,1,0:T(8,128)} %middle_y.1), calls=%async_computation.2 | async-start | bytes 262144 | tf_op jit(solution)/shard_map/all_to_all | solution.py:353
  95.3 4.2 %fusion.42 = f32[20,8,16,128]{3,2,1,0:T(8,128)S(1)} fusion(f32[20,8,16,128]{3,2,1,0:T(8,128)S(1)} %copy-done.22, f32[20,8,16,128]{3,2,1,0:T(8,128)S(1)} %copy-done.24, f32[20,1,16,128]{3,2,1,0:T(8,128)} %convert_element_type.47, f32[20,1,16,128]{3,2,1,0:T(8,128)} %convert_element_type.46, f32[20,8,16,127]{3,2,1,0:T(8,128)} %get-tuple-element.60, ...), kind=kLoop, calls=%fused_computation.50 | loop fusion | flops 13434880 | bytes 7675904 | tf_op jit(solution)/shard_map/add | solution.py:457
  103.0 7.5 %all-to-all-start.3 = ((bf16[32,12,128]{2,1,0:T(8,128)(2,1)}), bf16[32,12,128]{2,1,0:T(8,128)(2,1)S(1)}, u32[]{:S(2)}, u32[]{:S(2)}) async-start(bf16[32,12,128]{2,1,0:T(8,128)(2,1)} %backward_x.1), calls=%async_computation.3 | async-start | bytes 262144 | tf_op jit(solution)/shard_map/all_to_all | solution.py:360
  110.5 32.9 %while.10 = (s32[]{:T(128)}, f32[8,8,20,128]{3,2,1,0:T(8,128)}, bf16[8,8,20,128]{3,2,1,0:T(8,128)(2,1)}, bf16[800,20]{0,1:T(8,128)(2,1)S(1)}, bf16[400,800]{1,0:...) while((s32[]{:T(128)}, f32[8,8,20,128]{3,2,1,0:T(8,128)}, bf16[8,8,20,128]{3,2,1,0:T(8,128)(2,1)}, ...), condition=%wide.region_1.2_spmd, body=%wide.region_0.1_spmd.sunk | while | flops 715571200 | bytes 2551757 | solution.py:442
  110.5 3.2 %fusion.104 = bf16[8,400,128]{2,1,0:T(8,128)(2,1)S(1)} fusion(bf16[400,800]{1,0:T(8,128)(2,1)} %get-tuple-element.137, bf16[8,8,20,128]{3,2,1,0:T(8,128)(2,1)} %get-tuple-element.135, s32[]{:T(128)} %get-tuple-element.126, bf16[800,20]{0,1:T(8,128)(2,1)S(1)} %get-tuple-element.136), kind=kOutput, calls=%fused_computation.19.clone.1 | convolution fusion | flops 699187200 | bytes 1617664 | tf_op jit(solution)/shard_map/while/body/eval_jaxpr/kh,bhz->bkz/dot_general | solution.py:436
  114.6 3.2 %fusion.104 = bf16[8,400,128]{2,1,0:T(8,128)(2,1)S(1)} fusion(bf16[400,800]{1,0:T(8,128)(2,1)} %get-tuple-element.137, bf16[8,8,20,128]{3,2,1,0:T(8,128)(2,1)} %get-tuple-element.135, s32[]{:T(128)} %get-tuple-element.126, bf16[800,20]{0,1:T(8,128)(2,1)S(1)} %get-tuple-element.136), kind=kOutput, calls=%fused_computation.19.clone.1 | convolution fusion | flops 699187200 | bytes 1617664 | tf_op jit(solution)/shard_map/while/body/eval_jaxpr/kh,bhz->bkz/dot_general | solution.py:436
  118.7 3.2 %fusion.104 = bf16[8,400,128]{2,1,0:T(8,128)(2,1)S(1)} fusion(bf16[400,800]{1,0:T(8,128)(2,1)} %get-tuple-element.137, bf16[8,8,20,128]{3,2,1,0:T(8,128)(2,1)} %get-tuple-element.135, s32[]{:T(128)} %get-tuple-element.126, bf16[800,20]{0,1:T(8,128)(2,1)S(1)} %get-tuple-element.136), kind=kOutput, calls=%fused_computation.19.clone.1 | convolution fusion | flops 699187200 | bytes 1617664 | tf_op jit(solution)/shard_map/while/body/eval_jaxpr/kh,bhz->bkz/dot_general | solution.py:436
  122.8 3.2 %fusion.104 = bf16[8,400,128]{2,1,0:T(8,128)(2,1)S(1)} fusion(bf16[400,800]{1,0:T(8,128)(2,1)} %get-tuple-element.137, bf16[8,8,20,128]{3,2,1,0:T(8,128)(2,1)} %get-tuple-element.135, s32[]{:T(128)} %get-tuple-element.126, bf16[800,20]{0,1:T(8,128)(2,1)S(1)} %get-tuple-element.136), kind=kOutput, calls=%fused_computation.19.clone.1 | convolution fusion | flops 699187200 | bytes 1617664 | tf_op jit(solution)/shard_map/while/body/eval_jaxpr/kh,bhz->bkz/dot_general | solution.py:436
  126.9 3.2 %fusion.104 = bf16[8,400,128]{2,1,0:T(8,128)(2,1)S(1)} fusion(bf16[400,800]{1,0:T(8,128)(2,1)} %get-tuple-element.137, bf16[8,8,20,128]{3,2,1,0:T(8,128)(2,1)} %get-tuple-element.135, s32[]{:T(128)} %get-tuple-element.126, bf16[800,20]{0,1:T(8,128)(2,1)S(1)} %get-tuple-element.136), kind=kOutput, calls=%fused_computation.19.clone.1 | convolution fusion | flops 699187200 | bytes 1617664 | tf_op jit(solution)/shard_map/while/body/eval_jaxpr/kh,bhz->bkz/dot_general | solution.py:436
  131.0 3.2 %fusion.104 = bf16[8,400,128]{2,1,0:T(8,128)(2,1)S(1)} fusion(bf16[400,800]{1,0:T(8,128)(2,1)} %get-tuple-element.137, bf16[8,8,20,128]{3,2,1,0:T(8,128)(2,1)} %get-tuple-element.135, s32[]{:T(128)} %get-tuple-element.126, bf16[800,20]{0,1:T(8,128)(2,1)S(1)} %get-tuple-element.136), kind=kOutput, calls=%fused_computation.19.clone.1 | convolution fusion | flops 699187200 | bytes 1617664 | tf_op jit(solution)/shard_map/while/body/eval_jaxpr/kh,bhz->bkz/dot_general | solution.py:436
  135.1 3.2 %fusion.104 = bf16[8,400,128]{2,1,0:T(8,128)(2,1)S(1)} fusion(bf16[400,800]{1,0:T(8,128)(2,1)} %get-tuple-element.137, bf16[8,8,20,128]{3,2,1,0:T(8,128)(2,1)} %get-tuple-element.135, s32[]{:T(128)} %get-tuple-element.126, bf16[800,20]{0,1:T(8,128)(2,1)S(1)} %get-tuple-element.136), kind=kOutput, calls=%fused_computation.19.clone.1 | convolution fusion | flops 699187200 | bytes 1617664 | tf_op jit(solution)/shard_map/while/body/eval_jaxpr/kh,bhz->bkz/dot_general | solution.py:436
  139.2 3.2 %fusion.104 = bf16[8,400,128]{2,1,0:T(8,128)(2,1)S(1)} fusion(bf16[400,800]{1,0:T(8,128)(2,1)} %get-tuple-element.137, bf16[8,8,20,128]{3,2,1,0:T(8,128)(2,1)} %get-tuple-element.135, s32[]{:T(128)} %get-tuple-element.126, bf16[800,20]{0,1:T(8,128)(2,1)S(1)} %get-tuple-element.136), kind=kOutput, calls=%fused_computation.19.clone.1 | convolution fusion | flops 699187200 | bytes 1617664 | tf_op jit(solution)/shard_map/while/body/eval_jaxpr/kh,bhz->bkz/dot_general | solution.py:436
  143.3 6.0 %scatter_fusion = f32[20,128,128]{2,0,1:T(8,128)S(1)} fusion(f32[20,128,128]{2,0,1:T(8,128)S(1)} %bitcast.82, s32[64]{0:T(128)S(1)} %get-tuple-element.81, f32[64,20,128]{2,1,0:T(8,128)} %bitcast.88), kind=kCustom, calls=%fused_computation.1 | custom fusion | flops 163840 | bytes 1966336 | tf_op jit(solution)/shard_map/scatter-add | solution.py:468
  (137 shorter events, 42.0 us)
Async XLA Ops:
  0.6 25.7 %copy-start = (f32[3,8,16,128]{3,2,1,0:T(8,128)S(1)}, f32[3,8,16,128]{3,2,1,0:T(8,128)}, u32[]{:S(2)}) copy-start(f32[3,8,16,128]{3,2,1,0:T(8,128)} %param.31) | copy-start | bytes 589828
  0.7 25.7 %copy-start.1 = (bf16[128,128]{1,0:T(8,128)(2,1)S(1)}, bf16[128,128]{1,0:T(8,128)(2,1)}, u32[]{:S(2)}) copy-start(bf16[128,128]{1,0:T(8,128)(2,1)} %constant.102.clone.th) | copy-start | bytes 98308
  2.5 40.0 %collective-permute-start = (bf16[21,1,16,128]{3,2,1,0:T(8,128)(2,1)}, bf16[21,1,16,128]{3,2,1,0:T(8,128)(2,1)}, u32[]{:S(2)}, u32[]{:S(2)}) collective-permute-start(bf16[21,1,16,128]{3,2,1,0:T(8,128)(2,1)} %get-tuple-element.58), channel_id=1, source_target_pairs={{16,0},{32,16},{48,32},{64,48},{80,64},{96,80},{112,96},{128,112},... | collective-permute-start | bytes 258056 | tf_op jit(solution)/shard_map/ppermute | solution.py:379
  17.7 25.9 %collective-permute-start.1 = (bf16[21,1,16,128]{3,2,1,0:T(8,128)(2,1)}, bf16[21,1,16,128]{3,2,1,0:T(8,128)(2,1)}, u32[]{:S(2)}, u32[]{:S(2)}) collective-permute-start(bf16[21,1,16,128]{3,2,1,0:T(8,128)(2,1)} %get-tuple-element.57), channel_id=1, source_target_pairs={{0,16},{16,32},{32,48},{48,64},{64,80},{80,96},{96,112},{112,128},... | collective-permute-start | bytes 258056 | tf_op jit(solution)/shard_map/ppermute | solution.py:378
  20.4 20.0 %collective-permute-start.3 = (bf16[21,8,1,128]{3,2,1,0:T(2,128)(2,1)}, bf16[21,8,1,128]{3,2,1,0:T(2,128)(2,1)}, u32[]{:S(2)}, u32[]{:S(2)}) collective-permute-start(bf16[21,8,1,128]{3,2,1,0:T(2,128)(2,1)} %get-tuple-element.56), channel_id=1, source_target_pairs={{0,1},{1,2},{2,3},{3,4},{4,5},{5,6},{6,7},{7,8},{8,9},{9,10},{10,1... | collective-permute-start | bytes 129032 | tf_op jit(solution)/shard_map/ppermute | solution.py:378
  24.4 17.1 %collective-permute-start.2 = (bf16[21,8,1,128]{3,2,1,0:T(2,128)(2,1)}, bf16[21,8,1,128]{3,2,1,0:T(2,128)(2,1)}, u32[]{:S(2)}, u32[]{:S(2)}) collective-permute-start(bf16[21,8,1,128]{3,2,1,0:T(2,128)(2,1)} %get-tuple-element.55), channel_id=1, source_target_pairs={{1,0},{2,1},{3,2},{4,3},{5,4},{6,5},{7,6},{8,7},{9,8},{10,9},{11,1... | collective-permute-start | bytes 129032 | tf_op jit(solution)/shard_map/ppermute | solution.py:379
  27.4 31.1 %all-to-all-start = ((bf16[32,12,128]{2,1,0:T(8,128)(2,1)}), bf16[32,12,128]{2,1,0:T(8,128)(2,1)S(1)}, u32[]{:S(2)}, u32[]{:S(2)}) async-start(bf16[32,12,128]{2,1,0:T(8,128)(2,1)} %depth_modes.1), calls=%async_computation | async-start | bytes 262144 | tf_op jit(solution)/shard_map/all_to_all | solution.py:337
  52.4 26.4 %collective-permute-start.7 = (bf16[20,8,1,128]{3,2,1,0:T(2,128)(2,1)}, bf16[20,8,1,128]{3,2,1,0:T(2,128)(2,1)}, u32[]{:S(2)}, u32[]{:S(2)}) collective-permute-start(bf16[20,8,1,128]{3,2,1,0:T(2,128)(2,1)} %get-tuple-element.68), channel_id=1, source_target_pairs={{0,1},{1,2},{2,3},{3,4},{4,5},{5,6},{6,7},{7,8},{8,9},{9,10},{10,1... | collective-permute-start | bytes 122888 | tf_op jit(solution)/shard_map/ppermute | solution.py:378
  58.4 28.6 %copy-start.3 = (f32[32,8,128]{2,1,0:T(8,128)S(1)}, f32[32,8,128]{2,1,0:T(8,128)}, u32[]{:S(2)}) copy-start(f32[32,8,128]{2,1,0:T(8,128)} %constant.117.clone.ez) | copy-start | bytes 393220
  58.4 28.6 %copy-start.4 = (bf16[256,128]{1,0:T(8,128)(2,1)S(1)}, bf16[256,128]{1,0:T(8,128)(2,1)}, u32[]{:S(2)}) copy-start(bf16[256,128]{1,0:T(8,128)(2,1)} %constant.112.clone.th) | copy-start | bytes 196612
  58.4 28.6 %copy-start.5 = (bf16[256,128]{1,0:T(8,128)(2,1)S(1)}, bf16[256,128]{1,0:T(8,128)(2,1)}, u32[]{:S(2)}) copy-start(bf16[256,128]{1,0:T(8,128)(2,1)} %constant.113.clone.tl) | copy-start | bytes 196612
  58.4 28.6 %copy-start.6 = (bf16[128,256]{1,0:T(8,128)(2,1)S(1)}, bf16[128,256]{1,0:T(8,128)(2,1)}, u32[]{:S(2)}) copy-start(bf16[128,256]{1,0:T(8,128)(2,1)} %constant.114.clone.bh) | copy-start | bytes 196612
  58.4 28.6 %copy-start.7 = (bf16[128,256]{1,0:T(8,128)(2,1)S(1)}, bf16[128,256]{1,0:T(8,128)(2,1)}, u32[]{:S(2)}) copy-start(bf16[128,256]{1,0:T(8,128)(2,1)} %constant.115.clone.bl) | copy-start | bytes 196612
  58.4 28.6 %copy-start.8 = (f32[16,8,128]{2,1,0:T(8,128)S(1)}, f32[16,8,128]{2,1,0:T(8,128)}, u32[]{:S(2)}) copy-start(f32[16,8,128]{2,1,0:T(8,128)} %constant.116.clone.ex) | copy-start | bytes 196612
  58.4 28.6 %copy-start.19 = (f32[16,128]{1,0:T(8,128)S(1)}, f32[16,128]{1,0:T(8,128)}, u32[]{:S(2)}) copy-start(f32[16,128]{1,0:T(8,128)} %constant.110.clone.tc) | copy-start | bytes 24580
  58.4 28.6 %copy-start.20 = (f32[16,128]{1,0:T(8,128)S(1)}, f32[16,128]{1,0:T(8,128)}, u32[]{:S(2)}) copy-start(f32[16,128]{1,0:T(8,128)} %constant.111.clone.ts) | copy-start | bytes 24580
  58.5 28.6 %copy-start.21 = (f32[16,128]{1,0:T(8,128)S(1)}, f32[16,128]{1,0:T(8,128)}, u32[]{:S(2)}) copy-start(f32[16,128]{1,0:T(8,128)} %constant.118.clone.ey) | copy-start | bytes 24580
  59.6 35.7 %copy-start.24 = (f32[20,8,16,128]{3,2,1,0:T(8,128)S(1)}, f32[20,8,16,128]{3,2,1,0:T(8,128)}, u32[]{:S(2)}) copy-start(f32[20,8,16,128]{3,2,1,0:T(8,128)} %copy-done.23) | copy-start | bytes 3932164
  59.6 27.5 %all-to-all-start.1 = ((f32[16,16,128]{2,1,0:T(8,128)}), f32[16,16,128]{2,1,0:T(8,128)S(1)}, u32[]{:S(2)}, u32[]{:S(2)}) async-start(f32[16,16,128]{2,1,0:T(8,128)} %forward_x.1), calls=%async_computation.1 | async-start | bytes 262144 | tf_op jit(solution)/shard_map/all_to_all | solution.py:344
  66.8 16.6 %collective-permute-start.4 = (bf16[20,1,16,128]{3,2,1,0:T(8,128)(2,1)S(1)}, bf16[20,1,16,128]{3,2,1,0:T(8,128)(2,1)S(1)}, u32[]{:S(2)}, u32[]{:S(2)}) collective-permute-start(bf16[20,1,16,128]{3,2,1,0:T(8,128)(2,1)S(1)} %get-tuple-element.69), channel_id=1, source_target_pairs={{16,0},{32,16},{48,32},{64,48},{80,64},{96,80},{112,96},{128,112},... | collective-permute-start | bytes 245768 | tf_op jit(solution)/shard_map/ppermute | solution.py:379
  74.5 11.8 %collective-permute-start.5 = (bf16[20,1,16,128]{3,2,1,0:T(8,128)(2,1)S(1)}, bf16[20,1,16,128]{3,2,1,0:T(8,128)(2,1)S(1)}, u32[]{:S(2)}, u32[]{:S(2)}) collective-permute-start(bf16[20,1,16,128]{3,2,1,0:T(8,128)(2,1)S(1)} %get-tuple-element.70), channel_id=1, source_target_pairs={{0,16},{16,32},{32,48},{48,64},{64,80},{80,96},{96,112},{112,128},... | collective-permute-start | bytes 245768 | tf_op jit(solution)/shard_map/ppermute | solution.py:378
  76.5 6.1 %collective-permute-start.6 = (bf16[20,8,1,128]{3,2,1,0:T(2,128)(2,1)}, bf16[20,8,1,128]{3,2,1,0:T(2,128)(2,1)S(1)}, u32[]{:S(2)}, u32[]{:S(2)}) collective-permute-start(bf16[20,8,1,128]{3,2,1,0:T(2,128)(2,1)} %get-tuple-element.67), channel_id=1, source_target_pairs={{1,0},{2,1},{3,2},{4,3},{5,4},{6,5},{7,6},{8,7},{9,8},{10,9},{11,1... | collective-permute-start | bytes 122888 | tf_op jit(solution)/shard_map/ppermute | solution.py:379
  89.0 12.9 %all-to-all-start.2 = ((f32[16,16,128]{2,1,0:T(8,128)}), f32[16,16,128]{2,1,0:T(8,128)S(1)}, u32[]{:S(2)}, u32[]{:S(2)}) async-start(f32[16,16,128]{2,1,0:T(8,128)} %middle_y.1), calls=%async_computation.2 | async-start | bytes 262144 | tf_op jit(solution)/shard_map/all_to_all | solution.py:353
  103.0 47.6 %all-to-all-start.3 = ((bf16[32,12,128]{2,1,0:T(8,128)(2,1)}), bf16[32,12,128]{2,1,0:T(8,128)(2,1)S(1)}, u32[]{:S(2)}, u32[]{:S(2)}) async-start(bf16[32,12,128]{2,1,0:T(8,128)(2,1)} %backward_x.1), calls=%async_computation.3 | async-start | bytes 262144 | tf_op jit(solution)/shard_map/all_to_all | solution.py:360
  (29 other events, 235.3 us)

commit v2 on v1

v2 whole, which is shorter than its diff:
```python
import functools
import math

import jax
import jax.numpy as jnp
import numpy as np
from jax import lax
from jax.experimental import pallas as pl
from jax.experimental.pallas import tpu as pltpu
from jax.sharding import PartitionSpec as P


time_step = 0.25
early_slots = 16
f32 = jnp.float32
bf16 = jnp.bfloat16


def split_table(table):
    high = np.asarray(table, np.float64).astype(jnp.bfloat16)
    low = (np.asarray(table, np.float64) - high.astype(np.float64)).astype(jnp.bfloat16)
    return high, low


def product(left, right, contract):
    return lax.dot_general(left, right, (contract, ((), ())), preferred_element_type=f32)


def halves(value):
    high = value.astype(bf16)
    return high, (value - high.astype(f32)).astype(bf16)


def right_table(value, table_high, table_low):
    contract = ((1,), (0,))
    high, low = halves(value)
    return (
        product(high, table_high, contract)
        + product(low, table_high, contract)
        + product(high, table_low, contract)
    )


def times(pair, factor):
    real, imag = pair
    c, s = float(np.real(factor)), float(np.imag(factor))
    if abs(s) < 1e-12:
        return (real, imag) if c > 0 else (-real, -imag)
    if abs(c) < 1e-12:
        return (-imag, real) if s > 0 else (imag, -real)
    if abs(abs(c) - abs(s)) < 1e-12:
        size = abs(c)
        sc, ss = (1 if c > 0 else -1), (1 if s > 0 else -1)
        first = real * size
        second = imag * size
        new_real = (first if sc > 0 else -first) - (second if ss > 0 else -second)
        new_imag = (first if ss > 0 else -first) + (second if sc > 0 else -second)
        return new_real, new_imag
    return real * c - imag * s, real * s + imag * c


def complex_dft(values):
    count = len(values)
    if count == 1:
        return values
    even = complex_dft(values[0::2])
    odd = complex_dft(values[1::2])
    half = count // 2
    low, high = [], []
    for k in range(half):
        turned = times(odd[k], np.exp(-2j * np.pi * k / count))
        low.append((even[k][0] + turned[0], even[k][1] + turned[1]))
        high.append((even[k][0] - turned[0], even[k][1] - turned[1]))
    return low + high


def real_dft(values):
    count = len(values)
    if count == 2:
        zero = jnp.zeros_like(values[0])
        return [(values[0] + values[1], zero), (values[0] - values[1], zero)]
    even = real_dft(values[0::2])
    odd = real_dft(values[1::2])
    half = count // 2
    out = [None] * (half + 1)
    for k in range(half // 2 + 1):
        turned = times(odd[k], np.exp(-2j * np.pi * k / count))
        out[half - k] = (even[k][0] - turned[0], turned[1] - even[k][1])
        out[k] = (even[k][0] + turned[0], even[k][1] + turned[1])
    return out


def full_spectrum(values):
    half = real_dft(values)
    count = len(values)
    return [half[k] if k <= count // 2 else (half[count - k][0], -half[count - k][1]) for k in range(count)]


def turn(pair, cosine, sine):
    real, imag = pair
    return real * cosine + imag * sine, imag * cosine - real * sine


def lane_index(shape):
    return lax.broadcasted_iota(jnp.int32, shape, len(shape) - 1)


def central(values, step, roll):
    count = len(values)
    lane = lane_index(values[0].shape)
    if step == 16:
        digit, top = lane // 16, 7
        forward_from_other, backward_from_other = -16, 16
    else:
        digit, top = lane % 16, 15
        forward_from_other, backward_from_other = 15, -15
    last, first = digit == top, digit == 0
    up = [roll(v, -step) for v in values]
    down = [roll(v, step) for v in values]
    up_other = up if step == 16 else [roll(v, forward_from_other) for v in values]
    down_other = down if step == 16 else [roll(v, backward_from_other) for v in values]
    out = []
    for n in range(count):
        after = jnp.where(last, up_other[(n + 1) % count], up[n])
        before = jnp.where(first, down_other[(n - 1) % count], down[n])
        out.append(0.5 * (after - before))
    return out


def depth_modes(velocity, tables):
    plain, derived = tables
    fields = []
    for n in range(3):
        table_high, table_low = plain if n < 2 else derived
        high, low = halves(velocity[n])
        contract = ((1,), (1,))
        fields.append(
            product(table_high, high, contract)
            + product(table_high, low, contract)
            + product(table_low, high, contract)
        )
    return [
        jnp.concatenate([f[4 * n : 4 * n + 4] for f in fields], 0) for n in range(32)
    ]


def forward_x(values, turn_cos, turn_sin, roll):
    slope = central([v[0:8] for v in values], 16, roll)
    lines = [
        jnp.concatenate([s[0:4] + v[8:12], v[4:8]], 0) for s, v in zip(slope, values)
    ]
    modes = full_spectrum(lines)
    rows = []
    for k, pair in enumerate(modes):
        rows.append(jnp.concatenate(turn(pair, turn_cos[k : k + 1], turn_sin[k : k + 1]), 1))
    return jnp.concatenate(rows, 0)


def middle_y(values, fetch, roll):
    plain = [jnp.concatenate([v[0:4], v[8:12]], 0) for v in values]
    other = [jnp.concatenate([v[4:8], v[12:16]], 0) for v in values]
    lines = [p + s for p, s in zip(plain, central(other, 1, roll))]
    rows = []
    turns = fetch.get("turn")
    turn_cos, turn_sin, eigen_y = turns[:16], turns[16:32], turns[32:48]
    for k, pair in enumerate(full_spectrum(lines)):
        rows.append(jnp.concatenate(turn(pair, turn_cos[k : k + 1], turn_sin[k : k + 1]), 1))
    modes = right_table(jnp.concatenate(rows, 0), *split_pair(fetch.get("y")))
    eigen_xz = fetch.get("ex") + fetch.get("ez")
    scaled = []
    for k in range(16):
        eigen = eigen_xz + eigen_y[k : k + 1]
        mean_mode = eigen == 0.0
        scale = jnp.where(mean_mode, 0.0, (-1.0 / 65536.0) / jnp.where(mean_mode, 1.0, eigen))
        scaled.append(modes[8 * k : 8 * k + 8] * scale)
    back = right_table(jnp.concatenate(scaled, 0), *split_doubled(fetch.get("y_back")))
    pairs = []
    for k in range(16):
        row = back[8 * k : 8 * k + 8]
        pairs.append(turn((row[:, :128], row[:, 128:]), turn_cos[k : k + 1], turn_sin[k : k + 1]))
    pressure = [real - imag for real, imag in complex_dft(pairs)]
    slope = central(pressure, 1, roll)
    return [
        jnp.concatenate([p[0:4], s[0:4], p[4:8], s[4:8]], 0) for p, s in zip(pressure, slope)
    ]


def backward_x(modes, table_back, turn_cos, turn_sin, roll):
    back = right_table(modes, *table_back)
    pairs = []
    for k in range(32):
        row = back[8 * k : 8 * k + 8]
        pairs.append(turn((row[:, :128], row[:, 128:]), turn_cos[k : k + 1], turn_sin[k : k + 1]))
    lines = [real - imag for real, imag in complex_dft(pairs)]
    slope = central(lines, 16, roll)
    return [
        jnp.concatenate([s[0:4], v[4:8], v[0:4]], 0) for s, v in zip(slope, lines)
    ]


def depth_back(fields, tables):
    plain, derived = tables
    out = []
    for n in range(3):
        table_high, table_low = plain if n < 2 else derived
        turned = fields[n].T.astype(bf16)
        contract = ((1,), (0,))
        out.append(product(turned, table_high, contract) + product(turned, table_low, contract))
    return out


def cosine_numpy(length):
    position = np.arange(length)
    weight = np.where(position == 0, math.sqrt(1.0 / length), math.sqrt(2.0 / length))
    return weight[:, None] * np.cos(np.pi / (2 * length) * position[:, None] * (2 * position[None, :] + 1))


def make_tables():
    t = {}
    cosine = cosine_numpy(128)
    above = np.concatenate([cosine[:, 1:], cosine[:, -1:]], 1)
    below = np.concatenate([cosine[:, :1], cosine[:, :-1]], 1)
    t["depth"] = split_table(cosine)
    t["depth_back_slope"] = split_table(0.5 * (above - below))
    slope = np.zeros((128, 128))
    for z in range(128):
        slope[z, min(z + 1, 127)] += 0.5
        slope[z, max(z - 1, 0)] -= 0.5
    t["depth_slope"] = split_table(cosine @ slope)

    def digits(points):
        angle = 2 * np.pi / points * np.outer(np.arange(points), np.arange(points))
        return angle

    eight, sixteen = digits(8), digits(16)
    one16, one8 = np.eye(16), np.eye(8)
    t["x"] = split_table(
        np.concatenate(
            [np.kron(np.cos(eight) + np.sin(eight), one16), np.kron(np.sin(eight) - np.cos(eight), one16)], 0
        )
    )
    t["y"] = split_table(
        np.concatenate(
            [np.kron(one8, np.cos(sixteen) + np.sin(sixteen)), np.kron(one8, np.sin(sixteen) - np.cos(sixteen))], 0
        )
    )
    t["x_back"] = split_table(
        np.concatenate([np.kron(np.cos(eight), one16), np.kron(-np.sin(eight), one16)], 1)
    )
    t["y_back"] = split_table(
        np.concatenate([np.kron(one8, np.cos(sixteen)), np.kron(one8, -np.sin(sixteen))], 1)
    )
    lane = np.arange(128)
    turn_x = 2 * np.pi / 256 * np.outer(np.arange(32), lane // 16)
    turn_y = 2 * np.pi / 256 * np.outer(np.arange(16), lane % 16)
    t["turn_x"] = (np.cos(turn_x).astype(np.float32), np.sin(turn_x).astype(np.float32))
    t["turn_y"] = (np.cos(turn_y).astype(np.float32), np.sin(turn_y).astype(np.float32))
    k1 = np.arange(32)
    eigen_x = 2 - 2 * np.cos(2 * np.pi / 256 * (k1[:, None] + 32 * (lane // 16)[None, :]))
    t["eigen_x"] = np.repeat(eigen_x.reshape(16, 2, 128), 4, axis=1).astype(np.float32)
    kz = 2 - 2 * np.cos(np.pi * np.arange(128) / 128)
    t["eigen_z"] = np.ascontiguousarray(
        np.broadcast_to(np.tile(kz.reshape(32, 4), (1, 2))[:, :, None], (32, 8, 128))
    ).astype(np.float32)
    t["eigen_y"] = (
        2 - 2 * np.cos(2 * np.pi / 256 * (np.arange(16)[:, None] + 16 * (lane % 16)[None, :]))
    ).astype(np.float32)
    return t


def lane_roll(value, shift):
    return pltpu.roll(value, shift % 128, 1)


def pack_tables():
    t = make_tables()
    places, narrow, wide = {}, [], []
    at = 0
    for name in ("depth", "depth_slope", "depth_back_slope", "x", "y", "x_back", "y_back"):
        for n, table in enumerate(t[name]):
            if table.shape[1] == 256:
                table = np.concatenate([table[:, :128], table[:, 128:]], 0)
            places[name, n] = (at, at + table.shape[0])
            narrow.append(table)
            at += table.shape[0]
    at = 0
    for name in ("turn_x", "turn_y", "eigen_y", "eigen_x", "eigen_z"):
        parts = t[name] if isinstance(t[name], tuple) else (t[name],)
        for n, table in enumerate(parts):
            table = table.reshape(-1, 128)
            places[name, n] = (at, at + table.shape[0])
            wide.append(table)
            at += table.shape[0]
    return places, np.concatenate(narrow, 0), np.concatenate(wide, 0)


table_places, narrow_tables, wide_tables = pack_tables()


class Fetch:
    def __init__(self):
        self.copies = {}

    def start(self, name, source, target, flag):
        copy = pltpu.make_async_copy(source, target, flag)
        copy.start()
        self.copies[name] = (copy, target)

    def get(self, name):
        copy, target = self.copies[name]
        copy.wait()
        return target[...]


def rows_of(source, name, last=None):
    low = table_places[name, 0][0]
    high = max(b for (n, _), (_, b) in table_places.items() if n == (last or name))
    return source.at[pl.ds(low, high - low)]


def split_pair(table):
    half = table.shape[0] // 2
    return table[:half], table[half:]


def split_doubled(table):
    return tuple(jnp.concatenate([half[:128], half[128:]], 1) for half in split_pair(table))


def depth_kernel(velocity, narrow, out, one, flags):
    fetch = Fetch()
    fetch.start("depth", rows_of(narrow, "depth", "depth_slope"), one, flags.at[0])
    plain, derived = split_pair(fetch.get("depth"))
    groups = depth_modes([velocity[n] for n in range(3)], (split_pair(plain), split_pair(derived)))
    for n, group in enumerate(groups):
        out[n] = group.astype(bf16)


def forward_kernel(values, narrow, wide, out, one, two, flags):
    fetch = Fetch()
    fetch.start("turn", rows_of(wide, "turn_x"), two, flags.at[0])
    fetch.start("x", rows_of(narrow, "x"), one, flags.at[1])
    loaded = [values[n].astype(f32) for n in range(32)]
    rows = forward_x(loaded, *split_pair(fetch.get("turn")), lane_roll)
    modes = right_table(rows, *split_pair(fetch.get("x")))
    out[...] = modes.reshape(16, 16, 128)


def middle_kernel(values, narrow, wide, out, one, two, three, ex, ez, flags):
    fetch = Fetch()
    at_x = pl.multiple_of(table_places["eigen_x", 0][0] + 8 * lax.axis_index("gy"), 8)
    at_z = pl.multiple_of(table_places["eigen_z", 0][0] + 8 * lax.axis_index("gx"), 8)
    fetch.start("turn", rows_of(wide, "turn_y", "eigen_y"), three, flags.at[0])
    fetch.start("y", rows_of(narrow, "y"), one, flags.at[1])
    fetch.start("y_back", rows_of(narrow, "y_back"), two, flags.at[2])
    fetch.start("ex", wide.at[pl.ds(at_x, 8)], ex, flags.at[3])
    fetch.start("ez", wide.at[pl.ds(at_z, 8)], ez, flags.at[4])
    result = middle_y([values[n] for n in range(16)], fetch, lane_roll)
    for n, value in enumerate(result):
        out[n] = value


def backward_kernel(values, narrow, wide, out, one, two, flags):
    fetch = Fetch()
    fetch.start("x_back", rows_of(narrow, "x_back"), one, flags.at[0])
    fetch.start("turn", rows_of(wide, "turn_x"), two, flags.at[1])
    result = backward_x(
        values[...].reshape(256, 128),
        split_doubled(fetch.get("x_back")),
        *split_pair(fetch.get("turn")),
        lane_roll,
    )
    for n, value in enumerate(result):
        out[n] = value.astype(bf16)


def last_kernel(values, velocity, narrow, out, one, two, kept, flags):
    fetch = Fetch()
    fetch.start("depth", rows_of(narrow, "depth"), one, flags.at[0])
    fetch.start("slope", rows_of(narrow, "depth_back_slope"), two, flags.at[1])
    fetch.start("velocity", velocity, kept, flags.at[2])
    loaded = [values[n].astype(f32) for n in range(32)]
    fields = [jnp.concatenate([v[4 * n : 4 * n + 4] for v in loaded], 0) for n in range(3)]
    tables = (split_pair(fetch.get("depth")), split_pair(fetch.get("slope")))
    gradient = depth_back(fields, tables)
    velocity_before = fetch.get("velocity")
    for n, value in enumerate(gradient):
        out[n] = velocity_before[n] - value


def swap(modes, axis):
    return lax.all_to_all(modes, axis, split_axis=0, concat_axis=0, tiled=True)


def after(value, *others):
    return lax.optimization_barrier((value, *others))


near, far = pl.BlockSpec(memory_space=pltpu.VMEM), pl.BlockSpec(memory_space=pltpu.HBM)


def in_hbm(value):
    return pltpu.with_memory_space_constraint(value, pltpu.HBM)


def fetching(body, out_shape, operands, specs, rows, extra=()):
    scratch = [pltpu.VMEM((count, 128), kind) for count, kind in rows]
    scratch += list(extra) + [pltpu.SemaphoreType.DMA((len(rows) + len(extra),))]
    return pl.pallas_call(
        body,
        out_shape=out_shape,
        in_specs=specs,
        scratch_shapes=scratch,
        compiler_params=pltpu.CompilerParams(vmem_limit_bytes=16 << 20),
    )(*[in_hbm(value) if spec is far else value for value, spec in zip(operands, specs)])


def to_depth_modes(columns, narrow):
    shape = jax.ShapeDtypeStruct((32, 12, 128), bf16)
    return fetching(depth_kernel, shape, (columns, narrow), [near, far], [(512, bf16)])


def to_x_modes(modes, narrow, wide):
    shape = jax.ShapeDtypeStruct((16, 16, 128), f32)
    rows = [(512, bf16), (64, f32)]
    return fetching(forward_kernel, shape, (modes, narrow, wide), [near, far, far], rows)


def solve_y(modes, narrow, wide):
    shape = jax.ShapeDtypeStruct((16, 16, 128), f32)
    rows = [(512, bf16), (512, bf16), (48, f32), (8, f32), (8, f32)]
    return fetching(middle_kernel, shape, (modes, narrow, wide), [near, far, far], rows)


def from_x_modes(modes, narrow, wide):
    shape = jax.ShapeDtypeStruct((32, 12, 128), bf16)
    rows = [(512, bf16), (64, f32)]
    return fetching(backward_kernel, shape, (modes, narrow, wide), [near, far, far], rows)


def from_depth_modes(modes, columns, narrow):
    shape = jax.ShapeDtypeStruct((3, 128, 128), f32)
    rows = [(256, bf16), (256, bf16)]
    extra = [pltpu.VMEM((3, 128, 128), f32)]
    specs = [near, far, far]
    return fetching(last_kernel, shape, (modes, columns, narrow), specs, rows, extra)


def pack_y_kernel(s_far, v_far, k_far, up, down, v, s, k, flags):
    fetch = Fetch()
    fetch.start("s", s_far, s, flags.at[0])
    fetch.start("v", v_far, v, flags.at[1])
    fetch.start("k", k_far, k, flags.at[2])
    for copy, _ in fetch.copies.values():
        copy.wait()
    for side, near, far in ((up, 15, 14), (down, 0, 1)):
        for n in range(20):
            side[n] = s[pl.ds(n * 128 + near, 8, stride=16), :].astype(bf16)
            side[20 + n] = s[pl.ds(n * 128 + far, 8, stride=16), :].astype(bf16)
        side[40] = k[pl.ds(near, 8, stride=16), :].astype(bf16)
        side[41] = k[pl.ds(far, 8, stride=16), :].astype(bf16)
        for n in range(3):
            side[42 + n] = v[pl.ds(n * 128 + near, 8, stride=16), :].astype(bf16)
            side[45 + n] = jnp.zeros((8, 128), bf16)


def pack_x_kernel(s, v, k, ylow, yhigh, up, down, edge, corner):
    edge[0] = ylow[...].astype(f32).reshape(384, 128)
    edge[1] = yhigh[...].astype(f32).reshape(384, 128)
    for side, near, far in ((up, 7, 6), (down, 0, 1)):
        for n in range(20):
            side[n] = s[n * 128 + near * 16 : n * 128 + near * 16 + 16].astype(bf16)
            side[20 + n] = s[n * 128 + far * 16 : n * 128 + far * 16 + 16].astype(bf16)
        side[40] = k[near * 16 : near * 16 + 16].astype(bf16)
        side[41] = k[far * 16 : far * 16 + 16].astype(bf16)
        for n in range(3):
            side[42 + n] = v[n * 128 + near * 16 : n * 128 + near * 16 + 16].astype(bf16)
        for m in range(2):
            for n in range(20):
                corner[20 * m + n : 20 * m + n + 1] = edge[m, n * 8 + near : n * 8 + near + 1]
            corner[40 + m : 41 + m] = edge[m, 320 + near : 321 + near]
        corner[42:48] = jnp.zeros((6, 128), f32)
        for n in range(3):
            side[45 + n] = corner[16 * n : 16 * n + 16].astype(bf16)


def shifted(value, row, step):
    count = value.shape[0]
    index = lax.broadcasted_iota(jnp.int32, value.shape, 0)
    if step > 0:
        return jnp.where(index == count - 1, row, pltpu.roll(value, count - 1, 0))
    return jnp.where(index == 0, row, pltpu.roll(value, 1, 0))


def weights_of(k, kxn, kxp, kyn, kyp, u, v, w):
    lane = lane_index(k.shape)
    last, first = lane == 127, lane == 0
    kzn = jnp.where(last, k, pltpu.roll(k, 127, 1))
    kzp = jnp.where(first, k, pltpu.roll(k, 1, 1))
    eighth = 0.5 * time_step
    half = 0.5 * eighth * 2.0
    xn, xp = half * (k + kxn - u), half * (k + kxp + u)
    yn, yp = half * (k + kyn - v), half * (k + kyp + v)
    zn, zp = half * (k + kzn - w), half * (k + kzp + w)
    own = 1.0 - half * (6.0 * k + kxn + kxp + kyn + kyp + kzn + kzp)
    own = own + jnp.where(last, zn, 0.0) + jnp.where(first, zp, 0.0)
    return own, xn, xp, yn, yp, jnp.where(last, 0.0, zn), jnp.where(first, 0.0, zp)


def stepped(c, f, xn, xp, yn, yp):
    total = c[0] * f + c[1] * xn + c[2] * xp
    total = total + (c[3] * yn + c[4] * yp)
    return total + (c[5] * pltpu.roll(f, 127, 1) + c[6] * pltpu.roll(f, 1, 1))


def transport_kernel(s_far, v, k, ylow, yhigh, xlow, xhigh, out, s, yf, xf, cx, cy, flags):
    fetch = Fetch()
    fetch.start("s", s_far, s, flags.at[0])
    yf[0] = ylow[...].astype(f32).reshape(384, 128)
    yf[1] = yhigh[...].astype(f32).reshape(384, 128)
    xf[0] = xlow[...].astype(f32).reshape(768, 128)
    xf[1] = xhigh[...].astype(f32).reshape(768, 128)

    def plane(side, n):
        return xf[side, 16 * n : 16 * n + 16]

    def strip(side, n):
        return yf[side, 8 * n : 8 * n + 8]

    ks = [plane(0, 41), plane(0, 40)] + [k[16 * n : 16 * n + 16] for n in range(8)] + [plane(1, 40), plane(1, 41)]
    for p in range(10):
        if p == 0 or p == 9:
            side = 0 if p == 0 else 1
            flow = [plane(side, 42 + n) for n in range(3)]
            row_low, row_high = xf[side, 760:761], xf[side, 761:762]
        else:
            x = p - 1
            flow = [v[n * 128 + 16 * x : n * 128 + 16 * x + 16] for n in range(3)]
            row_low, row_high = yf[0, 320 + x : 321 + x], yf[1, 320 + x : 321 + x]
        own = ks[p + 1]
        made = weights_of(
            own, ks[p + 2], ks[p], shifted(own, row_high, 1), shifted(own, row_low, -1), *flow
        )
        for n in range(7):
            cx[p, n] = made[n]
    for side in range(2):
        own = strip(side, 40)
        inner = k[pl.ds(15 * side, 8, stride=16), :]
        around = (inner, strip(0, 41)) if side == 0 else (strip(1, 41), inner)
        made = weights_of(
            own,
            shifted(own, xf[1, 760 + side : 761 + side], 1),
            shifted(own, xf[0, 760 + side : 761 + side], -1),
            *around,
            *[strip(side, 42 + n) for n in range(3)],
        )
        for n in range(7):
            cy[side, n] = made[n]

    def channel(n, carry):
        base = pl.multiple_of(n * 128, 128)

        def far_plane(side, m):
            return xf[side, pl.ds(pl.multiple_of(m * 16, 16), 16), :]

        def far_strip(side, m):
            return yf[side, pl.ds(pl.multiple_of(m * 8, 8), 8), :]

        fields = [s[pl.ds(base + 16 * x, 16), :] for x in range(8)]
        planes = [far_plane(0, 20 + n), far_plane(0, n)] + fields + [far_plane(1, n), far_plane(1, 20 + n)]
        strips = [far_strip(side, n) for side in range(2)]
        far = [far_strip(side, 20 + n) for side in range(2)]
        corners = [[xf[side, pl.ds(720 + 20 * m + n, 1), :] for m in range(2)] for side in range(2)]
        section = []
        for p in range(10):
            if p == 0 or p == 9:
                row_low, row_high = corners[0 if p == 0 else 1]
            else:
                row_low, row_high = strips[0][p - 1 : p], strips[1][p - 1 : p]
            own = planes[p + 1]
            section.append(
                stepped(
                    [cx[p, m] for m in range(7)],
                    own,
                    planes[p + 2],
                    planes[p],
                    shifted(own, row_high, 1),
                    shifted(own, row_low, -1),
                )
            )
        edges = []
        for side in range(2):
            own = strips[side]
            inner = s[pl.ds(base + 15 * side, 8, stride=16), :]
            around = (inner, far[0]) if side == 0 else (far[1], inner)
            edges.append(
                stepped(
                    [cy[side, m] for m in range(7)],
                    own,
                    shifted(own, corners[1][side], 1),
                    shifted(own, corners[0][side], -1),
                    *around,
                )
            )
        for x in range(8):
            own = section[x + 1]
            moved = stepped(
                [cx[x + 1, m] for m in range(7)],
                own,
                section[x + 2],
                section[x],
                shifted(own, edges[1][x : x + 1], 1),
                shifted(own, edges[0][x : x + 1], -1),
            )
            out[pl.ds(base + 16 * x, 16), :] = 0.5 * (fields[x] + moved)
        return carry

    fetch.copies["s"][0].wait()
    lax.fori_loop(0, 20, channel, 0)


def gelu(x):
    inner = 0.7978845608028654 * (x + 0.044715 * (x * x * x))
    half = 0.5 * x
    return half + half * jnp.tanh(inner)


bundle = 4


def react_kernel(begin, end, listed, s, in_far, mid_far, out_far, out, w_in, w_mid, w_out, raw, flags):
    fetch = Fetch()
    fetch.start("in", in_far, raw, flags.at[0])
    fetch.start("mid", mid_far, w_mid, flags.at[1])
    fetch.start("out", out_far, w_out, flags.at[2])
    out[...] = s[...]
    w_in[...] = fetch.get("in").astype(f32).T.astype(bf16)
    for name in ("mid", "out"):
        fetch.copies[name][0].wait()

    def step(g, carry):
        first = g * bundle

        @pl.when(listed[first] < 128)
        def _():
            places = [listed[first + q] for q in range(bundle)]
            bounded = [jnp.minimum(place, 127) for place in places]
            rows = [s[pl.ds(place, 20, stride=128), :] for place in bounded]
            feed = jnp.concatenate(rows, 1).astype(bf16)
            one = gelu(product(w_in[...], feed, ((1,), (0,)))).astype(bf16)
            two = gelu(product(w_mid[...], one, ((1,), (0,)))).astype(bf16)
            change = product(w_out[...], two, ((1,), (0,)))
            for q in range(bundle):

                @pl.when(places[q] < 128)
                def _():
                    out[pl.ds(bounded[q], 20, stride=128), :] = (
                        rows[q] + change[:, 128 * q : 128 * q + 128]
                    )

        return carry

    lax.fori_loop(begin // bundle, end // bundle, step, 0)


def exchange(up, down, axis):
    size = lax.axis_size(axis)
    forward = [(n, (n + 1) % size) for n in range(size)]
    low = lax.ppermute(up, axis, forward)
    return low, lax.ppermute(down, axis, [(b, a) for a, b in forward])


def pack_y(s, v, k):
    strip = jax.ShapeDtypeStruct((48, 8, 128), bf16)
    return pl.pallas_call(
        pack_y_kernel,
        out_shape=(strip, strip, jax.ShapeDtypeStruct((384, 128), f32)),
        in_specs=[far] * 3,
        out_specs=(near,) * 3,
        scratch_shapes=[
            pltpu.VMEM((2560, 128), f32),
            pltpu.VMEM((128, 128), f32),
            pltpu.SemaphoreType.DMA((3,)),
        ],
        compiler_params=pltpu.CompilerParams(vmem_limit_bytes=16 << 20),
        name="pack_y",
    )(in_hbm(s), in_hbm(v), in_hbm(k))


def pack_x(s, v, k, ylow, yhigh):
    face = jax.ShapeDtypeStruct((48, 16, 128), bf16)
    return pl.pallas_call(
        pack_x_kernel,
        out_shape=(face, face),
        scratch_shapes=[pltpu.VMEM((2, 384, 128), f32), pltpu.VMEM((48, 128), f32)],
        compiler_params=pltpu.CompilerParams(vmem_limit_bytes=16 << 20),
        name="pack_x",
    )(s, v, k, ylow, yhigh)


def transport(s, v, k, strips, faces):
    return pl.pallas_call(
        transport_kernel,
        out_shape=jax.ShapeDtypeStruct((2560, 128), f32),
        in_specs=[far] + [near] * 6,
        scratch_shapes=[
            pltpu.VMEM((2560, 128), f32),
            pltpu.VMEM((2, 384, 128), f32),
            pltpu.VMEM((2, 768, 128), f32),
            pltpu.VMEM((10, 7, 16, 128), f32),
            pltpu.VMEM((2, 7, 8, 128), f32),
            pltpu.SemaphoreType.DMA((1,)),
        ],
        compiler_params=pltpu.CompilerParams(vmem_limit_bytes=24 << 20),
        name="transport",
    )(in_hbm(s), v, k, *strips, *faces)


def react(moved, listed, network, begin, end):
    w_in, w_mid, w_out = network
    return pl.pallas_call(
        functools.partial(react_kernel, begin, end),
        out_shape=jax.ShapeDtypeStruct((2560, 128), f32),
        in_specs=[pl.BlockSpec(memory_space=pltpu.SMEM), near, far, far, far],
        scratch_shapes=[
            pltpu.VMEM((800, 20), bf16),
            pltpu.VMEM((400, 800), bf16),
            pltpu.VMEM((20, 400), bf16),
            pltpu.VMEM((20, 800), bf16),
            pltpu.SemaphoreType.DMA((3,)),
        ],
        compiler_params=pltpu.CompilerParams(vmem_limit_bytes=32 << 20),
        name="react",
    )(listed, moved, in_hbm(w_in.T), in_hbm(w_mid), in_hbm(w_out))


def advance(scalars, velocity, diffusivity, burn_list, w_in, w_mid, w_out):
    s = scalars.reshape(2560, 128)
    v = velocity.reshape(384, 128)
    k = diffusivity.reshape(128, 128)
    listed = burn_list.reshape(64)
    up, down, kept = pack_y(s, v, k)
    narrow, wide = jnp.asarray(narrow_tables), jnp.asarray(wide_tables)
    network = (w_in, w_mid, w_out)
    strips = exchange(up, down, "gy")
    modes = to_depth_modes(kept.reshape(3, 128, 128), narrow)
    modes = swap(modes, "gx")
    up, down = pack_x(s, v, k, *strips)
    faces = exchange(up, down, "gx")
    modes, up, down = after(modes, up, down)
    modes = to_x_modes(modes, narrow, wide)
    modes = swap(modes, "gy")
    moved = transport(s, v, k, strips, faces)
    modes, moved = after(modes, moved)
    modes = swap(solve_y(modes, narrow, wide), "gy")
    moved = react(moved, listed, network, 0, early_slots)
    modes, moved = after(modes, moved)
    modes = swap(from_x_modes(modes, narrow, wide), "gx")
    moved = react(moved, listed, network, early_slots, 64)
    velocity_out = from_depth_modes(modes, velocity.reshape(3, 128, 128), narrow)
    return (moved.reshape(scalars.shape), velocity_out.reshape(velocity.shape))


def solution(mesh):
    in_specs = (
        P(None, "gx", "gy", None),
        P(None, "gx", "gy", None),
        P("gx", "gy", None),
        P("gx", "gy", None),
        P(),
        P(),
        P(),
    )
    out_specs = (P(None, "gx", "gy", None), P(None, "gx", "gy", None))
    return jax.shard_map(advance, mesh=mesh, in_specs=in_specs, out_specs=out_specs, check_vma=False)
```

time: 153 us -> 113 us (0.74)
  Pallas kernels: 6.01 us -> 44.5 us
  matrix products: 32.8 us -> 0 us
  other arithmetic: 27.2 us -> 0 us
  local copies, waits for them, and re-layouts: 13 us -> 0.02 us
  starting transfers between devices: 66.6 us -> 54.1 us
  waiting for transfers between devices: 4.54 us -> 12.9 us
    pallas_call x5 -> x10, Pallas kernels: 6.01 us -> 44.5 us  [the longest x2 27.8 us: react(): pl.pallas_call(functools.partial(react_kernel, begin, end), out_shape=jax...]
    dot_general x16 -> x0, matrix products: 32.8 us -> none  [the longest x8 25.8 us: evaluate(): jnp.einsum('kh,bhz->bkz', w_mid, hidden_one, preferred_element_type=jnp.f...]
    ppermute x8 -> x4, starting transfers between devices: 39 us -> 15.4 us  [the longest x2 8.57 us: exchange(): return (low, lax.ppermute(down, axis, [(b, a) for a, b in forward]))]
    all_to_all x4, starting transfers between devices: 27.6 us -> 38.7 us  [swap(): return lax.all_to_all(modes, axis, split_axis=0, concat_axis=0, tiled=True)]
    slice x8 -> x0, local copies, waits for them, and re-layouts: 10.1 us -> none  [the longest x6 8.35 us: depth_next(): return jnp.concatenate([values[..., 1:], values[..., -1:]], -1)]
    ppermute x8 -> x4, waiting for transfers between devices: 4.52 us -> 11.9 us  [the longest x2 8.83 us: exchange(): return (low, lax.ppermute(down, axis, [(b, a) for a, b in forward]))]
    scatter-add x1 -> x0, other arithmetic: 5.96 us -> none  [shards(): flat_blocks.at[:, listed]]
    another operation x2 -> x0, other arithmetic: 4.82 us -> none
  transfers between devices with their start and end apart: 12 -> 8, of which waited for: 2 -> 4; matrix products, arithmetic and copies ran while one was open for 47% -> 0% of each run, Pallas kernels for 1% -> 29%
where the time goes in v2:
time: 113 us; the launch traced here: 112 us
  starting transfers between devices  54.1 us (48%)
  Pallas kernels  44.5 us (39%)
  waiting for transfers between devices  12.9 us (11%)
    all_to_all x4, starting transfers between devices, swap(): return lax.all_to_all(modes, axis, split_axis=0, concat_axis=0, tiled=True)  38.7 us
    pallas_call x2, Pallas kernels, react(): pl.pallas_call(functools.partial(react_kernel, begin, end), out_shape=jax...  27.8 us
    pallas_call x5, Pallas kernels, fetching(): pl.pallas_call(body, out_shape=out_shape, in_specs=specs, scratch_shapes=...  9.94 us
    ppermute x2, waiting for transfers between devices, exchange(): return (low, lax.ppermute(down, axis, [(b, a) for a, b in forward]))  8.83 us
    ppermute x2, starting transfers between devices, exchange(): return (low, lax.ppermute(down, axis, [(b, a) for a, b in forward]))  8.57 us
    ppermute x2, starting transfers between devices, exchange(): low = lax.ppermute(up, axis, forward)  6.8 us
    pallas_call x1, Pallas kernels, transport(): pl.pallas_call(transport_kernel, out_shape=jax.ShapeDtypeStruct((2560, 12...  5.06 us
    ppermute x2, waiting for transfers between devices, exchange(): low = lax.ppermute(up, axis, forward)  3.04 us
  transfers between devices with their start and end apart: 8, of which 4 were waited for; matrix products, arithmetic and copies ran while one was open for 0% of the time, Pallas kernels for 29%

profile of v2, /device:TPU:1, one launch (start us, length us, event | category | flops | bytes accessed | tf_op | source)
XLA Modules:
  0.0 112.3 jit_solution(12318190165969501516)
XLA Ops:
  0.6 0.0 copy-start
  0.7 1.6 %pack_y.1 = (bf16[48,8,128]{2,1,0:T(8,128)(2,1)S(1)}, bf16[48,8,128]{2,1,0:T(8,128)(2,1)S(1)}, f32[384,128]{1,0:T(8,128)S(1)}) custom-call(f32[2560,128]{1,0:T(8,128)} %bitcast.9, f32[384,128]{1,0:T(8,128)} %bitcast.12, f32[128,128]{1,0:T(8,128)} %bitcast.16), custom_call_target="tpu_custom_call" | custom-call | tf_op jit(solution)/shard_map/pack_y/pallas_call | solution.py:675
  2.3 1.9 %shard_map.104 = bf16[32,12,128]{2,1,0:T(8,128)(2,1)} custom-call(f32[3,128,128]{2,1,0:T(8,128)S(1)} %bitcast.19, bf16[2816,128]{1,0:T(8,128)(2,1)} %constant.4.clone.narrow), custom_call_target="tpu_custom_call" | custom-call | tf_op jit(solution)/shard_map/pallas_call | solution.py:409
  4.2 16.5 %all-to-all-start = ((bf16[32,12,128]{2,1,0:T(8,128)(2,1)}), bf16[32,12,128]{2,1,0:T(8,128)(2,1)S(1)}, u32[]{:S(2)}, u32[]{:S(2)}) async-start(bf16[32,12,128]{2,1,0:T(8,128)(2,1)} %shard_map.104), calls=%async_computation | async-start | bytes 262144 | tf_op jit(solution)/shard_map/all_to_all | solution.py:392
  20.7 4.0 %collective-permute-start = (bf16[48,8,128]{2,1,0:T(8,128)(2,1)S(1)}, bf16[48,8,128]{2,1,0:T(8,128)(2,1)S(1)}, u32[]{:S(2)}, u32[]{:S(2)}) collective-permute-start(bf16[48,8,128]{2,1,0:T(8,128)(2,1)S(1)} %get-tuple-element.13), channel_id=1, source_target_pairs={{0,1},{1,2},{2,3},{3,4},{4,5},{5,6},{6,7},{7,8},{8,9},{9,10},{10,1... | collective-permute-start | bytes 294920 | tf_op jit(solution)/shard_map/ppermute | solution.py:669
  24.7 1.9 %collective-permute-start.1 = (bf16[48,8,128]{2,1,0:T(8,128)(2,1)S(1)}, bf16[48,8,128]{2,1,0:T(8,128)(2,1)S(1)}, u32[]{:S(2)}, u32[]{:S(2)}) collective-permute-start(bf16[48,8,128]{2,1,0:T(8,128)(2,1)S(1)} %get-tuple-element.14), channel_id=1, source_target_pairs={{1,0},{2,1},{3,2},{4,3},{5,4},{6,5},{7,6},{8,7},{9,8},{10,9},{11,1... | collective-permute-start | bytes 294920 | tf_op jit(solution)/shard_map/ppermute | solution.py:670
  26.6 4.3 %collective-permute-done.1.yhigh = bf16[48,8,128]{2,1,0:T(8,128)(2,1)S(1)} collective-permute-done((bf16[48,8,128]{2,1,0:T(8,128)(2,1)S(1)}, bf16[48,8,128]{2,1,0:T(8,128)(2,1)S(1)}, u32[]{:S(2)}, u32[]{:S(2)}) %collective-permute-start.1) | collective-permute-done | bytes 98336 | tf_op jit(solution)/shard_map/ppermute | solution.py:670
  30.9 0.1 pack_x.1
  31.0 1.0 all-to-all-done.values
  32.0 1.9 %shard_map.105 = f32[16,16,128]{2,1,0:T(8,128)} custom-call(bf16[32,12,128]{2,1,0:T(8,128)(2,1)S(1)} %all-to-all-done.values, bf16[2816,128]{1,0:T(8,128)(2,1)} %constant.4.clone.narrow, f32[496,128]{1,0:T(8,128)} %constant.5.clone.wide), custom_call_target="tpu_custom_call" | custom-call | tf_op jit(solution)/shard_map/pallas_call | solution.py:409
  33.9 6.5 %all-to-all-start.1 = ((f32[16,16,128]{2,1,0:T(8,128)}), f32[16,16,128]{2,1,0:T(8,128)S(1)}, u32[]{:S(2)}, u32[]{:S(2)}) async-start(f32[16,16,128]{2,1,0:T(8,128)} %shard_map.105), calls=%async_computation.1 | async-start | bytes 262144 | tf_op jit(solution)/shard_map/all_to_all | solution.py:392
  40.4 2.8 %collective-permute-start.2 = (bf16[48,16,128]{2,1,0:T(8,128)(2,1)S(1)}, bf16[48,16,128]{2,1,0:T(8,128)(2,1)S(1)}, u32[]{:S(2)}, u32[]{:S(2)}) collective-permute-start(bf16[48,16,128]{2,1,0:T(8,128)(2,1)S(1)} %get-tuple-element.15), channel_id=1, source_target_pairs={{0,16},{16,32},{32,48},{48,64},{64,80},{80,96},{96,112},{112,128},... | collective-permute-start | bytes 589832 | tf_op jit(solution)/shard_map/ppermute | solution.py:669
  43.2 6.6 %collective-permute-start.3 = (bf16[48,16,128]{2,1,0:T(8,128)(2,1)S(1)}, bf16[48,16,128]{2,1,0:T(8,128)(2,1)S(1)}, u32[]{:S(2)}, u32[]{:S(2)}) collective-permute-start(bf16[48,16,128]{2,1,0:T(8,128)(2,1)S(1)} %get-tuple-element.16), channel_id=1, source_target_pairs={{16,0},{32,16},{48,32},{64,48},{80,64},{96,80},{112,96},{128,112},... | collective-permute-start | bytes 589832 | tf_op jit(solution)/shard_map/ppermute | solution.py:670
  49.9 3.0 %collective-permute-done.2.xlow = bf16[48,16,128]{2,1,0:T(8,128)(2,1)S(1)} collective-permute-done((bf16[48,16,128]{2,1,0:T(8,128)(2,1)S(1)}, bf16[48,16,128]{2,1,0:T(8,128)(2,1)S(1)}, u32[]{:S(2)}, u32[]{:S(2)}) %collective-permute-start.2) | collective-permute-done | bytes 196640 | tf_op jit(solution)/shard_map/ppermute | solution.py:669
  52.9 4.5 %collective-permute-done.3.xhigh = bf16[48,16,128]{2,1,0:T(8,128)(2,1)S(1)} collective-permute-done((bf16[48,16,128]{2,1,0:T(8,128)(2,1)S(1)}, bf16[48,16,128]{2,1,0:T(8,128)(2,1)S(1)}, u32[]{:S(2)}, u32[]{:S(2)}) %collective-permute-start.3) | collective-permute-done | bytes 196640 | tf_op jit(solution)/shard_map/ppermute | solution.py:670
  57.5 5.1 %transport.1.s = f32[2560,128]{1,0:T(8,128)S(1)} custom-call(f32[2560,128]{1,0:T(8,128)} %bitcast.10, f32[384,128]{1,0:T(8,128)S(1)} %bitcast.15, f32[128,128]{1,0:T(8,128)S(1)} %bitcast.18, bf16[48,8,128]{2,1,0:T(8,128)(2,1)S(1)} %collective-permute-done.ylow, bf16[48,8,128]{2,1,0:T(8,128)(2,1)S(1)} %collective-permute-done.1.yhigh, ...), custom_call_target="tpu_custom_call" | custom-call | tf_op jit(solution)/shard_map/transport/pallas_call | solution.py:702
  62.5 0.0 copy-start.3
  62.5 2.3 %shard_map.106 = f32[16,16,128]{2,1,0:T(8,128)} custom-call(f32[16,16,128]{2,1,0:T(8,128)S(1)} %all-to-all-done.1.values, bf16[2816,128]{1,0:T(8,128)(2,1)} %constant.4.clone.narrow, f32[496,128]{1,0:T(8,128)} %constant.5.clone.wide), custom_call_target="tpu_custom_call" | custom-call | tf_op jit(solution)/shard_map/pallas_call | solution.py:409
  64.8 6.1 %all-to-all-start.2 = ((f32[16,16,128]{2,1,0:T(8,128)}), f32[16,16,128]{2,1,0:T(8,128)S(1)}, u32[]{:S(2)}, u32[]{:S(2)}) async-start(f32[16,16,128]{2,1,0:T(8,128)} %shard_map.106), calls=%async_computation.2 | async-start | bytes 262144 | tf_op jit(solution)/shard_map/all_to_all | solution.py:392
  71.0 7.5 %react.2.s = f32[2560,128]{1,0:T(8,128)S(1)} custom-call(s32[64]{0:T(128)S(1)} %bitcast.20, f32[2560,128]{1,0:T(8,128)S(1)} %transport.1.s, bf16[20,800]{1,0:T(8,128)(2,1)} %bitcast.24, bf16[400,800]{1,0:T(8,128)(2,1)} %mid_far.3, bf16[20,400]{1,0:T(8,128)(2,1)} %out_far.3), custom_call_target="tpu_custom_call" | custom-call | tf_op jit(solution)/shard_map/react/pallas_call | solution.py:721
  78.5 2.0 %shard_map.107 = bf16[32,12,128]{2,1,0:T(8,128)(2,1)} custom-call(f32[16,16,128]{2,1,0:T(8,128)S(1)} %all-to-all-done.2.values, bf16[2816,128]{1,0:T(8,128)(2,1)} %constant.4.clone.narrow, f32[496,128]{1,0:T(8,128)} %constant.5.clone.wide), custom_call_target="tpu_custom_call" | custom-call | tf_op jit(solution)/shard_map/pallas_call | solution.py:409
  80.5 9.6 %all-to-all-start.3 = ((bf16[32,12,128]{2,1,0:T(8,128)(2,1)}), bf16[32,12,128]{2,1,0:T(8,128)(2,1)S(1)}, u32[]{:S(2)}, u32[]{:S(2)}) async-start(bf16[32,12,128]{2,1,0:T(8,128)(2,1)} %shard_map.107), calls=%async_computation.3 | async-start | bytes 262144 | tf_op jit(solution)/shard_map/all_to_all | solution.py:392
  90.1 20.3 %react.3 = f32[2560,128]{1,0:T(8,128)} custom-call(s32[64]{0:T(128)S(1)} %bitcast.21, f32[2560,128]{1,0:T(8,128)S(1)} %react.2.s, bf16[20,800]{1,0:T(8,128)(2,1)} %bitcast.25, bf16[400,800]{1,0:T(8,128)(2,1)} %mid_far.3, bf16[20,400]{1,0:T(8,128)(2,1)} %out_far.3), custom_call_target="tpu_custom_call" | custom-call | tf_op jit(solution)/shard_map/react/pallas_call | solution.py:721
  110.4 1.9 %shard_map.108 = f32[3,128,128]{2,1,0:T(8,128)} custom-call(bf16[32,12,128]{2,1,0:T(8,128)(2,1)S(1)} %all-to-all-done.3.values, f32[3,128,128]{2,1,0:T(8,128)} %bitcast.13, bf16[2816,128]{1,0:T(8,128)(2,1)} %constant.4.clone.narrow), custom_call_target="tpu_custom_call" | custom-call | tf_op jit(solution)/shard_map/pallas_call | solution.py:409
  (10 shorter events, 0.0 us)
Async XLA Ops:
  0.6 30.3 %copy-start = (f32[20,8,16,128]{3,2,1,0:T(8,128)S(1)}, f32[20,8,16,128]{3,2,1,0:T(8,128)}, u32[]{:S(2)}) copy-start(f32[20,8,16,128]{3,2,1,0:T(8,128)} %param.9) | copy-start | bytes 3932164
  0.6 30.3 %copy-start.1 = (f32[3,8,16,128]{3,2,1,0:T(8,128)S(1)}, f32[3,8,16,128]{3,2,1,0:T(8,128)}, u32[]{:S(2)}) copy-start(f32[3,8,16,128]{3,2,1,0:T(8,128)} %param.10) | copy-start | bytes 589828
  0.7 30.3 %copy-start.2 = (f32[8,16,128]{2,1,0:T(8,128)S(1)}, f32[8,16,128]{2,1,0:T(8,128)}, u32[]{:S(2)}) copy-start(f32[8,16,128]{2,1,0:T(8,128)} %param.11) | copy-start | bytes 196612
  4.2 27.9 %all-to-all-start = ((bf16[32,12,128]{2,1,0:T(8,128)(2,1)}), bf16[32,12,128]{2,1,0:T(8,128)(2,1)S(1)}, u32[]{:S(2)}, u32[]{:S(2)}) async-start(bf16[32,12,128]{2,1,0:T(8,128)(2,1)} %shard_map.104), calls=%async_computation | async-start | bytes 262144 | tf_op jit(solution)/shard_map/all_to_all | solution.py:392
  20.7 5.9 %collective-permute-start = (bf16[48,8,128]{2,1,0:T(8,128)(2,1)S(1)}, bf16[48,8,128]{2,1,0:T(8,128)(2,1)S(1)}, u32[]{:S(2)}, u32[]{:S(2)}) collective-permute-start(bf16[48,8,128]{2,1,0:T(8,128)(2,1)S(1)} %get-tuple-element.13), channel_id=1, source_target_pairs={{0,1},{1,2},{2,3},{3,4},{4,5},{5,6},{6,7},{7,8},{8,9},{9,10},{10,1... | collective-permute-start | bytes 294920 | tf_op jit(solution)/shard_map/ppermute | solution.py:669
  24.7 6.2 %collective-permute-start.1 = (bf16[48,8,128]{2,1,0:T(8,128)(2,1)S(1)}, bf16[48,8,128]{2,1,0:T(8,128)(2,1)S(1)}, u32[]{:S(2)}, u32[]{:S(2)}) collective-permute-start(bf16[48,8,128]{2,1,0:T(8,128)(2,1)S(1)} %get-tuple-element.14), channel_id=1, source_target_pairs={{1,0},{2,1},{3,2},{4,3},{5,4},{6,5},{7,6},{8,7},{9,8},{10,9},{11,1... | collective-permute-start | bytes 294920 | tf_op jit(solution)/shard_map/ppermute | solution.py:670
  33.9 28.6 %all-to-all-start.1 = ((f32[16,16,128]{2,1,0:T(8,128)}), f32[16,16,128]{2,1,0:T(8,128)S(1)}, u32[]{:S(2)}, u32[]{:S(2)}) async-start(f32[16,16,128]{2,1,0:T(8,128)} %shard_map.105), calls=%async_computation.1 | async-start | bytes 262144 | tf_op jit(solution)/shard_map/all_to_all | solution.py:392
  40.4 12.5 %collective-permute-start.2 = (bf16[48,16,128]{2,1,0:T(8,128)(2,1)S(1)}, bf16[48,16,128]{2,1,0:T(8,128)(2,1)S(1)}, u32[]{:S(2)}, u32[]{:S(2)}) collective-permute-start(bf16[48,16,128]{2,1,0:T(8,128)(2,1)S(1)} %get-tuple-element.15), channel_id=1, source_target_pairs={{0,16},{16,32},{32,48},{48,64},{64,80},{80,96},{96,112},{112,128},... | collective-permute-start | bytes 589832 | tf_op jit(solution)/shard_map/ppermute | solution.py:669
  43.2 14.2 %collective-permute-start.3 = (bf16[48,16,128]{2,1,0:T(8,128)(2,1)S(1)}, bf16[48,16,128]{2,1,0:T(8,128)(2,1)S(1)}, u32[]{:S(2)}, u32[]{:S(2)}) collective-permute-start(bf16[48,16,128]{2,1,0:T(8,128)(2,1)S(1)} %get-tuple-element.16), channel_id=1, source_target_pairs={{16,0},{32,16},{48,32},{64,48},{80,64},{96,80},{112,96},{128,112},... | collective-permute-start | bytes 589832 | tf_op jit(solution)/shard_map/ppermute | solution.py:670
  62.5 8.4 %copy-start.3 = (s32[1,1,64]{2,1,0:T(1,128)S(1)}, s32[1,1,64]{2,1,0:T(1,128)}, u32[]{:S(2)}) copy-start(s32[1,1,64]{2,1,0:T(1,128)} %param.12) | copy-start | bytes 772
  64.8 13.7 %all-to-all-start.2 = ((f32[16,16,128]{2,1,0:T(8,128)}), f32[16,16,128]{2,1,0:T(8,128)S(1)}, u32[]{:S(2)}, u32[]{:S(2)}) async-start(f32[16,16,128]{2,1,0:T(8,128)} %shard_map.106), calls=%async_computation.2 | async-start | bytes 262144 | tf_op jit(solution)/shard_map/all_to_all | solution.py:392
  80.5 29.9 %all-to-all-start.3 = ((bf16[32,12,128]{2,1,0:T(8,128)(2,1)}), bf16[32,12,128]{2,1,0:T(8,128)(2,1)S(1)}, u32[]{:S(2)}, u32[]{:S(2)}) async-start(bf16[32,12,128]{2,1,0:T(8,128)(2,1)} %shard_map.107), calls=%async_computation.3 | async-start | bytes 262144 | tf_op jit(solution)/shard_map/all_to_all | solution.py:392

commit v3 on v2

--- a/solution.py
+++ b/solution.py
@@ -272,6 +272,14 @@
     return pltpu.roll(value, shift % 128, 1)
 
 
+def call(body, out_shape, operands, limit=16):
+    return pl.pallas_call(
+        body,
+        out_shape=out_shape,
+        compiler_params=pltpu.CompilerParams(vmem_limit_bytes=limit << 20),
+    )(*operands)
+
+
 def pack_tables():
     t = make_tables()
     places, narrow, wide = {}, [], []
@@ -327,22 +335,17 @@
     return tuple(jnp.concatenate([half[:128], half[128:]], 1) for half in split_pair(table))
 
 
-def depth_kernel(velocity, narrow, out, one, flags):
-    fetch = Fetch()
-    fetch.start("depth", rows_of(narrow, "depth", "depth_slope"), one, flags.at[0])
-    plain, derived = split_pair(fetch.get("depth"))
+def depth_kernel(velocity, table, out):
+    plain, derived = split_pair(table[...])
     groups = depth_modes([velocity[n] for n in range(3)], (split_pair(plain), split_pair(derived)))
     for n, group in enumerate(groups):
         out[n] = group.astype(bf16)
 
 
-def forward_kernel(values, narrow, wide, out, one, two, flags):
-    fetch = Fetch()
-    fetch.start("turn", rows_of(wide, "turn_x"), two, flags.at[0])
-    fetch.start("x", rows_of(narrow, "x"), one, flags.at[1])
+def forward_kernel(values, table, turns, out):
     loaded = [values[n].astype(f32) for n in range(32)]
-    rows = forward_x(loaded, *split_pair(fetch.get("turn")), lane_roll)
-    modes = right_table(rows, *split_pair(fetch.get("x")))
+    rows = forward_x(loaded, *split_pair(turns[...]), lane_roll)
+    modes = right_table(rows, *split_pair(table[...]))
     out[...] = modes.reshape(16, 16, 128)
 
 
@@ -374,15 +377,13 @@
         out[n] = value.astype(bf16)
 
 
-def last_kernel(values, velocity, narrow, out, one, two, kept, flags):
+def last_kernel(values, velocity, table, out, kept, flags):
     fetch = Fetch()
-    fetch.start("depth", rows_of(narrow, "depth"), one, flags.at[0])
-    fetch.start("slope", rows_of(narrow, "depth_back_slope"), two, flags.at[1])
-    fetch.start("velocity", velocity, kept, flags.at[2])
+    fetch.start("velocity", velocity, kept, flags.at[0])
     loaded = [values[n].astype(f32) for n in range(32)]
     fields = [jnp.concatenate([v[4 * n : 4 * n + 4] for v in loaded], 0) for n in range(3)]
-    tables = (split_pair(fetch.get("depth")), split_pair(fetch.get("slope")))
-    gradient = depth_back(fields, tables)
+    plain, derived = split_pair(table[...])
+    gradient = depth_back(fields, (split_pair(plain), split_pair(derived)))
     velocity_before = fetch.get("velocity")
     for n, value in enumerate(gradient):
         out[n] = velocity_before[n] - value
@@ -415,15 +416,23 @@
     )(*[in_hbm(value) if spec is far else value for value, spec in zip(operands, specs)])
 
 
-def to_depth_modes(columns, narrow):
+def table_rows(source, *names):
+    found = []
+    for name in names:
+        high = max(b for (n, _), (_, b) in table_places.items() if n == name)
+        found.append(source[table_places[name, 0][0] : high])
+    return jnp.asarray(np.concatenate(found, 0))
+
+
+def to_depth_modes(columns):
     shape = jax.ShapeDtypeStruct((32, 12, 128), bf16)
-    return fetching(depth_kernel, shape, (columns, narrow), [near, far], [(512, bf16)])
-
-
-def to_x_modes(modes, narrow, wide):
+    return call(depth_kernel, shape, (columns, table_rows(narrow_tables, "depth", "depth_slope")))
+
+
+def to_x_modes(modes):
     shape = jax.ShapeDtypeStruct((16, 16, 128), f32)
-    rows = [(512, bf16), (64, f32)]
-    return fetching(forward_kernel, shape, (modes, narrow, wide), [near, far, far], rows)
+    tables = (table_rows(narrow_tables, "x"), table_rows(wide_tables, "turn_x"))
+    return call(forward_kernel, shape, (modes, *tables))
 
 
 def solve_y(modes, narrow, wide):
@@ -438,12 +447,11 @@
     return fetching(backward_kernel, shape, (modes, narrow, wide), [near, far, far], rows)
 
 
-def from_depth_modes(modes, columns, narrow):
+def from_depth_modes(modes, columns):
     shape = jax.ShapeDtypeStruct((3, 128, 128), f32)
-    rows = [(256, bf16), (256, bf16)]
+    table = table_rows(narrow_tables, "depth", "depth_back_slope")
     extra = [pltpu.VMEM((3, 128, 128), f32)]
-    specs = [near, far, far]
-    return fetching(last_kernel, shape, (modes, columns, narrow), specs, rows, extra)
+    return fetching(last_kernel, shape, (modes, columns, table), [near, far, near], [], extra)
 
 
 def pack_y_kernel(s_far, v_far, k_far, up, down, v, s, k, flags):
@@ -619,24 +627,24 @@
     lax.fori_loop(0, 20, channel, 0)
 
 
-def gelu(x):
-    inner = 0.7978845608028654 * (x + 0.044715 * (x * x * x))
-    half = 0.5 * x
-    return half + half * jnp.tanh(inner)
-
-
-bundle = 4
-
-
-def react_kernel(begin, end, listed, s, in_far, mid_far, out_far, out, w_in, w_mid, w_out, raw, flags):
+def gelu_doubled(x):
+    return x + x * jnp.tanh(x * (0.7978845608028654 + 0.035677408136300125 * (x * x)))
+
+
+bundle = 16
+
+
+def react_kernel(begin, end, listed, s, in_far, mid_far, out_far, out, w_in, w_mid, w_out, *rest):
+    raw_in, raw_mid, raw_out, flags = rest
     fetch = Fetch()
-    fetch.start("in", in_far, raw, flags.at[0])
-    fetch.start("mid", mid_far, w_mid, flags.at[1])
-    fetch.start("out", out_far, w_out, flags.at[2])
+    fetch.start("in", in_far, raw_in, flags.at[0])
+    fetch.start("mid", mid_far, raw_mid, flags.at[1])
+    fetch.start("out", out_far, raw_out, flags.at[2])
     out[...] = s[...]
     w_in[...] = fetch.get("in").astype(f32).T.astype(bf16)
-    for name in ("mid", "out"):
-        fetch.copies[name][0].wait()
+    half = jnp.asarray(0.5, bf16)
+    w_mid[...] = fetch.get("mid") * half
+    w_out[...] = fetch.get("out") * half
 
     def step(g, carry):
         first = g * bundle
@@ -647,8 +655,8 @@
             bounded = [jnp.minimum(place, 127) for place in places]
             rows = [s[pl.ds(place, 20, stride=128), :] for place in bounded]
             feed = jnp.concatenate(rows, 1).astype(bf16)
-            one = gelu(product(w_in[...], feed, ((1,), (0,)))).astype(bf16)
-            two = gelu(product(w_mid[...], one, ((1,), (0,)))).astype(bf16)
+            one = gelu_doubled(product(w_in[...], feed, ((1,), (0,)))).astype(bf16)
+            two = gelu_doubled(product(w_mid[...], one, ((1,), (0,)))).astype(bf16)
             change = product(w_out[...], two, ((1,), (0,)))
             for q in range(bundle):
 
@@ -727,9 +735,11 @@
             pltpu.VMEM((400, 800), bf16),
             pltpu.VMEM((20, 400), bf16),
             pltpu.VMEM((20, 800), bf16),
+            pltpu.VMEM((400, 800), bf16),
+            pltpu.VMEM((20, 400), bf16),
             pltpu.SemaphoreType.DMA((3,)),
         ],
-        compiler_params=pltpu.CompilerParams(vmem_limit_bytes=32 << 20),
+        compiler_params=pltpu.CompilerParams(vmem_limit_bytes=48 << 20),
         name="react",
     )(listed, moved, in_hbm(w_in.T), in_hbm(w_mid), in_hbm(w_out))
 
@@ -743,12 +753,12 @@
     narrow, wide = jnp.asarray(narrow_tables), jnp.asarray(wide_tables)
     network = (w_in, w_mid, w_out)
     strips = exchange(up, down, "gy")
-    modes = to_depth_modes(kept.reshape(3, 128, 128), narrow)
+    modes = to_depth_modes(kept.reshape(3, 128, 128))
     modes = swap(modes, "gx")
     up, down = pack_x(s, v, k, *strips)
     faces = exchange(up, down, "gx")
     modes, up, down = after(modes, up, down)
-    modes = to_x_modes(modes, narrow, wide)
+    modes = to_x_modes(modes)
     modes = swap(modes, "gy")
     moved = transport(s, v, k, strips, faces)
     modes, moved = after(modes, moved)
@@ -757,7 +767,7 @@
     modes, moved = after(modes, moved)
     modes = swap(from_x_modes(modes, narrow, wide), "gx")
     moved = react(moved, listed, network, early_slots, 64)
-    velocity_out = from_depth_modes(modes, velocity.reshape(3, 128, 128), narrow)
+    velocity_out = from_depth_modes(modes, velocity.reshape(3, 128, 128))
     return (moved.reshape(scalars.shape), velocity_out.reshape(velocity.shape))
 
 

time: 113 us -> 104 us (0.920)
  Pallas kernels: 44.5 us -> 34.7 us
    pallas_call x2, Pallas kernels: 27.8 us -> 19.9 us  [react(): pl.pallas_call(functools.partial(react_kernel, begin, end), out_shape=jax...]
    pallas_call x5 -> x3, Pallas kernels: 9.94 us -> 6.05 us  [fetching(): pl.pallas_call(body, out_shape=out_shape, in_specs=specs, scratch_shapes=...]
    pallas_call x0 -> x2, Pallas kernels: none -> 2.04 us  [call(): pl.pallas_call(body, out_shape=out_shape, compiler_params=pltpu.CompilerP...]
  transfers between devices with their start and end apart: 8 -> 8, of which waited for: 4 -> 5; matrix products, arithmetic and copies ran while one was open for 0% -> 0% of each run, Pallas kernels for 29% -> 24%
where the time goes in v3:
time: 104 us; the launch traced here: 103 us
  starting transfers between devices  54 us (52%)
  Pallas kernels  34.7 us (33%)
  waiting for transfers between devices  13.4 us (13%)
    all_to_all x4, starting transfers between devices, swap(): return lax.all_to_all(modes, axis, split_axis=0, concat_axis=0, tiled=True)  38.6 us
    pallas_call x2, Pallas kernels, react(): pl.pallas_call(functools.partial(react_kernel, begin, end), out_shape=jax...  19.9 us
    ppermute x2, waiting for transfers between devices, exchange(): return (low, lax.ppermute(down, axis, [(b, a) for a, b in forward]))  8.84 us
    ppermute x2, starting transfers between devices, exchange(): return (low, lax.ppermute(down, axis, [(b, a) for a, b in forward]))  8.57 us
    ppermute x2, starting transfers between devices, exchange(): low = lax.ppermute(up, axis, forward)  6.8 us
    pallas_call x3, Pallas kernels, fetching(): pl.pallas_call(body, out_shape=out_shape, in_specs=specs, scratch_shapes=...  6.05 us
    pallas_call x1, Pallas kernels, transport(): pl.pallas_call(transport_kernel, out_shape=jax.ShapeDtypeStruct((2560, 12...  5.06 us
    ppermute x2, waiting for transfers between devices, exchange(): low = lax.ppermute(up, axis, forward)  3.04 us
  transfers between devices with their start and end apart: 8, of which 5 were waited for; matrix products, arithmetic and copies ran while one was open for 0% of the time, Pallas kernels for 24%

profile of v3, /device:TPU:1, one launch (start us, length us, event | category | flops | bytes accessed | tf_op | source)
XLA Modules:
  0.0 103.0 jit_solution(3554179914819272948)
XLA Ops:
  0.7 1.6 %pack_y.1 = (bf16[48,8,128]{2,1,0:T(8,128)(2,1)S(1)}, bf16[48,8,128]{2,1,0:T(8,128)(2,1)S(1)}, f32[384,128]{1,0:T(8,128)S(1)}) custom-call(f32[2560,128]{1,0:T(8,128)} %bitcast.9, f32[384,128]{1,0:T(8,128)} %bitcast.12, f32[128,128]{1,0:T(8,128)} %bitcast.16), custom_call_target="tpu_custom_call" | custom-call | tf_op jit(solution)/shard_map/pack_y/pallas_call | solution.py:683
  2.3 0.0 copy-start.5
  2.3 1.0 shard_map.140
  3.3 16.5 %all-to-all-start = ((bf16[32,12,128]{2,1,0:T(8,128)(2,1)}), bf16[32,12,128]{2,1,0:T(8,128)(2,1)S(1)}, u32[]{:S(2)}, u32[]{:S(2)}) async-start(bf16[32,12,128]{2,1,0:T(8,128)(2,1)} %shard_map.140), calls=%async_computation | async-start | bytes 262144 | tf_op jit(solution)/shard_map/all_to_all | solution.py:393
  19.8 4.0 %collective-permute-start = (bf16[48,8,128]{2,1,0:T(8,128)(2,1)S(1)}, bf16[48,8,128]{2,1,0:T(8,128)(2,1)S(1)}, u32[]{:S(2)}, u32[]{:S(2)}) collective-permute-start(bf16[48,8,128]{2,1,0:T(8,128)(2,1)S(1)} %get-tuple-element.13), channel_id=1, source_target_pairs={{0,1},{1,2},{2,3},{3,4},{4,5},{5,6},{6,7},{7,8},{8,9},{9,10},{10,1... | collective-permute-start | bytes 294920 | tf_op jit(solution)/shard_map/ppermute | solution.py:677
  23.8 1.9 %collective-permute-start.1 = (bf16[48,8,128]{2,1,0:T(8,128)(2,1)S(1)}, bf16[48,8,128]{2,1,0:T(8,128)(2,1)S(1)}, u32[]{:S(2)}, u32[]{:S(2)}) collective-permute-start(bf16[48,8,128]{2,1,0:T(8,128)(2,1)S(1)} %get-tuple-element.14), channel_id=1, source_target_pairs={{1,0},{2,1},{3,2},{4,3},{5,4},{6,5},{7,6},{8,7},{9,8},{10,9},{11,1... | collective-permute-start | bytes 294920 | tf_op jit(solution)/shard_map/ppermute | solution.py:678
  25.7 4.3 %collective-permute-done.1.yhigh = bf16[48,8,128]{2,1,0:T(8,128)(2,1)S(1)} collective-permute-done((bf16[48,8,128]{2,1,0:T(8,128)(2,1)S(1)}, bf16[48,8,128]{2,1,0:T(8,128)(2,1)S(1)}, u32[]{:S(2)}, u32[]{:S(2)}) %collective-permute-start.1) | collective-permute-done | bytes 98336 | tf_op jit(solution)/shard_map/ppermute | solution.py:678
  30.0 0.1 pack_x.1
  30.1 1.0 all-to-all-done.values
  31.2 1.0 %shard_map.141 = f32[16,16,128]{2,1,0:T(8,128)} custom-call(bf16[32,12,128]{2,1,0:T(8,128)(2,1)S(1)} %all-to-all-done.values, bf16[512,128]{1,0:T(8,128)(2,1)S(1)} %copy-done.5, f32[64,128]{1,0:T(8,128)S(1)} %copy-done.6), custom_call_target="tpu_custom_call" | custom-call | tf_op jit(solution)/shard_map/pallas_call | solution.py:276
  32.2 6.5 %all-to-all-start.1 = ((f32[16,16,128]{2,1,0:T(8,128)}), f32[16,16,128]{2,1,0:T(8,128)S(1)}, u32[]{:S(2)}, u32[]{:S(2)}) async-start(f32[16,16,128]{2,1,0:T(8,128)} %shard_map.141), calls=%async_computation.1 | async-start | bytes 262144 | tf_op jit(solution)/shard_map/all_to_all | solution.py:393
  38.7 2.8 %collective-permute-start.2 = (bf16[48,16,128]{2,1,0:T(8,128)(2,1)S(1)}, bf16[48,16,128]{2,1,0:T(8,128)(2,1)S(1)}, u32[]{:S(2)}, u32[]{:S(2)}) collective-permute-start(bf16[48,16,128]{2,1,0:T(8,128)(2,1)S(1)} %get-tuple-element.15), channel_id=1, source_target_pairs={{0,16},{16,32},{32,48},{48,64},{64,80},{80,96},{96,112},{112,128},... | collective-permute-start | bytes 589832 | tf_op jit(solution)/shard_map/ppermute | solution.py:677
  41.5 6.6 %collective-permute-start.3 = (bf16[48,16,128]{2,1,0:T(8,128)(2,1)S(1)}, bf16[48,16,128]{2,1,0:T(8,128)(2,1)S(1)}, u32[]{:S(2)}, u32[]{:S(2)}) collective-permute-start(bf16[48,16,128]{2,1,0:T(8,128)(2,1)S(1)} %get-tuple-element.16), channel_id=1, source_target_pairs={{16,0},{32,16},{48,32},{64,48},{80,64},{96,80},{112,96},{128,112},... | collective-permute-start | bytes 589832 | tf_op jit(solution)/shard_map/ppermute | solution.py:678
  48.2 3.0 %collective-permute-done.2.xlow = bf16[48,16,128]{2,1,0:T(8,128)(2,1)S(1)} collective-permute-done((bf16[48,16,128]{2,1,0:T(8,128)(2,1)S(1)}, bf16[48,16,128]{2,1,0:T(8,128)(2,1)S(1)}, u32[]{:S(2)}, u32[]{:S(2)}) %collective-permute-start.2) | collective-permute-done | bytes 196640 | tf_op jit(solution)/shard_map/ppermute | solution.py:677
  51.2 4.6 %collective-permute-done.3.xhigh = bf16[48,16,128]{2,1,0:T(8,128)(2,1)S(1)} collective-permute-done((bf16[48,16,128]{2,1,0:T(8,128)(2,1)S(1)}, bf16[48,16,128]{2,1,0:T(8,128)(2,1)S(1)}, u32[]{:S(2)}, u32[]{:S(2)}) %collective-permute-start.3) | collective-permute-done | bytes 196640 | tf_op jit(solution)/shard_map/ppermute | solution.py:678
  55.8 5.1 %transport.1.s = f32[2560,128]{1,0:T(8,128)S(1)} custom-call(f32[2560,128]{1,0:T(8,128)} %bitcast.10, f32[384,128]{1,0:T(8,128)S(1)} %bitcast.15, f32[128,128]{1,0:T(8,128)S(1)} %bitcast.18, bf16[48,8,128]{2,1,0:T(8,128)(2,1)S(1)} %collective-permute-done.ylow, bf16[48,8,128]{2,1,0:T(8,128)(2,1)S(1)} %collective-permute-done.1.yhigh, ...), custom_call_target="tpu_custom_call" | custom-call | tf_op jit(solution)/shard_map/transport/pallas_call | solution.py:710
  60.9 2.3 %shard_map.142 = f32[16,16,128]{2,1,0:T(8,128)} custom-call(f32[16,16,128]{2,1,0:T(8,128)S(1)} %all-to-all-done.1.values, bf16[2816,128]{1,0:T(8,128)(2,1)} %constant.12.clone.narrow, f32[496,128]{1,0:T(8,128)} %constant.13.clone.wide), custom_call_target="tpu_custom_call" | custom-call | tf_op jit(solution)/shard_map/pallas_call | solution.py:410
  63.1 6.1 %all-to-all-start.2 = ((f32[16,16,128]{2,1,0:T(8,128)}), f32[16,16,128]{2,1,0:T(8,128)S(1)}, u32[]{:S(2)}, u32[]{:S(2)}) async-start(f32[16,16,128]{2,1,0:T(8,128)} %shard_map.142), calls=%async_computation.2 | async-start | bytes 262144 | tf_op jit(solution)/shard_map/all_to_all | solution.py:393
  69.2 5.6 %react.2.s = f32[2560,128]{1,0:T(8,128)S(1)} custom-call(s32[64]{0:T(128)S(1)} %bitcast.20, f32[2560,128]{1,0:T(8,128)S(1)} %transport.1.s, bf16[20,800]{1,0:T(8,128)(2,1)} %bitcast.24, bf16[400,800]{1,0:T(8,128)(2,1)} %mid_far.3, bf16[20,400]{1,0:T(8,128)(2,1)} %out_far.3), custom_call_target="tpu_custom_call" | custom-call | tf_op jit(solution)/shard_map/react/pallas_call | solution.py:729
  74.8 0.5 all-to-all-done.2.values
  75.4 2.0 %shard_map.143 = bf16[32,12,128]{2,1,0:T(8,128)(2,1)} custom-call(f32[16,16,128]{2,1,0:T(8,128)S(1)} %all-to-all-done.2.values, bf16[2816,128]{1,0:T(8,128)(2,1)} %constant.12.clone.narrow, f32[496,128]{1,0:T(8,128)} %constant.13.clone.wide), custom_call_target="tpu_custom_call" | custom-call | tf_op jit(solution)/shard_map/pallas_call | solution.py:410
  77.4 9.6 %all-to-all-start.3 = ((bf16[32,12,128]{2,1,0:T(8,128)(2,1)}), bf16[32,12,128]{2,1,0:T(8,128)(2,1)S(1)}, u32[]{:S(2)}, u32[]{:S(2)}) async-start(bf16[32,12,128]{2,1,0:T(8,128)(2,1)} %shard_map.143), calls=%async_computation.3 | async-start | bytes 262144 | tf_op jit(solution)/shard_map/all_to_all | solution.py:393
  87.0 14.3 %react.3 = f32[2560,128]{1,0:T(8,128)} custom-call(s32[64]{0:T(128)S(1)} %bitcast.21, f32[2560,128]{1,0:T(8,128)S(1)} %react.2.s, bf16[20,800]{1,0:T(8,128)(2,1)} %bitcast.25, bf16[400,800]{1,0:T(8,128)(2,1)} %mid_far.3, bf16[20,400]{1,0:T(8,128)(2,1)} %out_far.3), custom_call_target="tpu_custom_call" | custom-call | tf_op jit(solution)/shard_map/react/pallas_call | solution.py:729
  101.3 1.7 %shard_map.144 = f32[3,128,128]{2,1,0:T(8,128)} custom-call(bf16[32,12,128]{2,1,0:T(8,128)(2,1)S(1)} %all-to-all-done.3.values, f32[3,128,128]{2,1,0:T(8,128)} %bitcast.13, bf16[512,128]{1,0:T(8,128)(2,1)S(1)} %copy-done.3), custom_call_target="tpu_custom_call" | custom-call | tf_op jit(solution)/shard_map/pallas_call | solution.py:410
  (18 shorter events, 0.1 us)
Async XLA Ops:
  0.6 1.7 %copy-start.4 = (bf16[512,128]{1,0:T(8,128)(2,1)S(1)}, bf16[512,128]{1,0:T(8,128)(2,1)}, u32[]{:S(2)}) copy-start(bf16[512,128]{1,0:T(8,128)(2,1)} %constant.14.clone.table) | copy-start | bytes 393220
  0.6 29.4 %copy-start.1 = (f32[3,8,16,128]{3,2,1,0:T(8,128)S(1)}, f32[3,8,16,128]{3,2,1,0:T(8,128)}, u32[]{:S(2)}) copy-start(f32[3,8,16,128]{3,2,1,0:T(8,128)} %param.14) | copy-start | bytes 589828
  0.7 29.4 %copy-start.2 = (f32[8,16,128]{2,1,0:T(8,128)S(1)}, f32[8,16,128]{2,1,0:T(8,128)}, u32[]{:S(2)}) copy-start(f32[8,16,128]{2,1,0:T(8,128)} %param.15) | copy-start | bytes 196612
  0.7 29.4 %copy-start = (f32[20,8,16,128]{3,2,1,0:T(8,128)S(1)}, f32[20,8,16,128]{3,2,1,0:T(8,128)}, u32[]{:S(2)}) copy-start(f32[20,8,16,128]{3,2,1,0:T(8,128)} %param.13) | copy-start | bytes 3932164
  2.3 28.9 %copy-start.5 = (bf16[512,128]{1,0:T(8,128)(2,1)S(1)}, bf16[512,128]{1,0:T(8,128)(2,1)}, u32[]{:S(2)}) copy-start(bf16[512,128]{1,0:T(8,128)(2,1)} %constant.15.clone.table) | copy-start | bytes 393220
  2.3 28.9 %copy-start.6 = (f32[64,128]{1,0:T(8,128)S(1)}, f32[64,128]{1,0:T(8,128)}, u32[]{:S(2)}) copy-start(f32[64,128]{1,0:T(8,128)} %constant.16.clone.turns) | copy-start | bytes 98308
  3.3 27.8 %all-to-all-start = ((bf16[32,12,128]{2,1,0:T(8,128)(2,1)}), bf16[32,12,128]{2,1,0:T(8,128)(2,1)S(1)}, u32[]{:S(2)}, u32[]{:S(2)}) async-start(bf16[32,12,128]{2,1,0:T(8,128)(2,1)} %shard_map.140), calls=%async_computation | async-start | bytes 262144 | tf_op jit(solution)/shard_map/all_to_all | solution.py:393
  19.8 5.9 %collective-permute-start = (bf16[48,8,128]{2,1,0:T(8,128)(2,1)S(1)}, bf16[48,8,128]{2,1,0:T(8,128)(2,1)S(1)}, u32[]{:S(2)}, u32[]{:S(2)}) collective-permute-start(bf16[48,8,128]{2,1,0:T(8,128)(2,1)S(1)} %get-tuple-element.13), channel_id=1, source_target_pairs={{0,1},{1,2},{2,3},{3,4},{4,5},{5,6},{6,7},{7,8},{8,9},{9,10},{10,1... | collective-permute-start | bytes 294920 | tf_op jit(solution)/shard_map/ppermute | solution.py:677
  23.8 6.2 %collective-permute-start.1 = (bf16[48,8,128]{2,1,0:T(8,128)(2,1)S(1)}, bf16[48,8,128]{2,1,0:T(8,128)(2,1)S(1)}, u32[]{:S(2)}, u32[]{:S(2)}) collective-permute-start(bf16[48,8,128]{2,1,0:T(8,128)(2,1)S(1)} %get-tuple-element.14), channel_id=1, source_target_pairs={{1,0},{2,1},{3,2},{4,3},{5,4},{6,5},{7,6},{8,7},{9,8},{10,9},{11,1... | collective-permute-start | bytes 294920 | tf_op jit(solution)/shard_map/ppermute | solution.py:678
  32.2 28.6 %all-to-all-start.1 = ((f32[16,16,128]{2,1,0:T(8,128)}), f32[16,16,128]{2,1,0:T(8,128)S(1)}, u32[]{:S(2)}, u32[]{:S(2)}) async-start(f32[16,16,128]{2,1,0:T(8,128)} %shard_map.141), calls=%async_computation.1 | async-start | bytes 262144 | tf_op jit(solution)/shard_map/all_to_all | solution.py:393
  38.7 12.5 %collective-permute-start.2 = (bf16[48,16,128]{2,1,0:T(8,128)(2,1)S(1)}, bf16[48,16,128]{2,1,0:T(8,128)(2,1)S(1)}, u32[]{:S(2)}, u32[]{:S(2)}) collective-permute-start(bf16[48,16,128]{2,1,0:T(8,128)(2,1)S(1)} %get-tuple-element.15), channel_id=1, source_target_pairs={{0,16},{16,32},{32,48},{48,64},{64,80},{80,96},{96,112},{112,128},... | collective-permute-start | bytes 589832 | tf_op jit(solution)/shard_map/ppermute | solution.py:677
  41.5 14.2 %collective-permute-start.3 = (bf16[48,16,128]{2,1,0:T(8,128)(2,1)S(1)}, bf16[48,16,128]{2,1,0:T(8,128)(2,1)S(1)}, u32[]{:S(2)}, u32[]{:S(2)}) collective-permute-start(bf16[48,16,128]{2,1,0:T(8,128)(2,1)S(1)} %get-tuple-element.16), channel_id=1, source_target_pairs={{16,0},{32,16},{48,32},{64,48},{80,64},{96,80},{112,96},{128,112},... | collective-permute-start | bytes 589832 | tf_op jit(solution)/shard_map/ppermute | solution.py:678
  60.8 8.4 %copy-start.7 = (s32[1,1,64]{2,1,0:T(1,128)S(1)}, s32[1,1,64]{2,1,0:T(1,128)}, u32[]{:S(2)}) copy-start(s32[1,1,64]{2,1,0:T(1,128)} %param.16) | copy-start | bytes 772
  63.1 12.2 %all-to-all-start.2 = ((f32[16,16,128]{2,1,0:T(8,128)}), f32[16,16,128]{2,1,0:T(8,128)S(1)}, u32[]{:S(2)}, u32[]{:S(2)}) async-start(f32[16,16,128]{2,1,0:T(8,128)} %shard_map.142), calls=%async_computation.2 | async-start | bytes 262144 | tf_op jit(solution)/shard_map/all_to_all | solution.py:393
  77.4 23.9 %all-to-all-start.3 = ((bf16[32,12,128]{2,1,0:T(8,128)(2,1)}), bf16[32,12,128]{2,1,0:T(8,128)(2,1)S(1)}, u32[]{:S(2)}, u32[]{:S(2)}) async-start(bf16[32,12,128]{2,1,0:T(8,128)(2,1)} %shard_map.143), calls=%async_computation.3 | async-start | bytes 262144 | tf_op jit(solution)/shard_map/all_to_all | solution.py:393
  87.0 14.3 %copy-start.3 = (bf16[512,128]{1,0:T(8,128)(2,1)S(1)}, bf16[512,128]{1,0:T(8,128)(2,1)}, u32[]{:S(2)}) copy-start(bf16[512,128]{1,0:T(8,128)(2,1)} %constant.17.clone.table) | copy-start | bytes 393220

commit v4 on v3

--- a/solution.py
+++ b/solution.py
@@ -320,12 +320,6 @@
         return target[...]
 
 
-def rows_of(source, name, last=None):
-    low = table_places[name, 0][0]
-    high = max(b for (n, _), (_, b) in table_places.items() if n == (last or name))
-    return source.at[pl.ds(low, high - low)]
-
-
 def split_pair(table):
     half = table.shape[0] // 2
     return table[:half], table[half:]
@@ -349,44 +343,41 @@
     out[...] = modes.reshape(16, 16, 128)
 
 
-def middle_kernel(values, narrow, wide, out, one, two, three, ex, ez, flags):
+class Held:
+    def __init__(self, fetch, **held):
+        self.fetch, self.held = fetch, held
+
+    def get(self, name):
+        return self.held[name][...] if name in self.held else self.fetch.get(name)
+
+
+def middle_kernel(values, table, back, turns, wide, out, ex, ez, flags):
     fetch = Fetch()
     at_x = pl.multiple_of(table_places["eigen_x", 0][0] + 8 * lax.axis_index("gy"), 8)
     at_z = pl.multiple_of(table_places["eigen_z", 0][0] + 8 * lax.axis_index("gx"), 8)
-    fetch.start("turn", rows_of(wide, "turn_y", "eigen_y"), three, flags.at[0])
-    fetch.start("y", rows_of(narrow, "y"), one, flags.at[1])
-    fetch.start("y_back", rows_of(narrow, "y_back"), two, flags.at[2])
-    fetch.start("ex", wide.at[pl.ds(at_x, 8)], ex, flags.at[3])
-    fetch.start("ez", wide.at[pl.ds(at_z, 8)], ez, flags.at[4])
-    result = middle_y([values[n] for n in range(16)], fetch, lane_roll)
+    fetch.start("ex", wide.at[pl.ds(at_x, 8)], ex, flags.at[0])
+    fetch.start("ez", wide.at[pl.ds(at_z, 8)], ez, flags.at[1])
+    tables = Held(fetch, y=table, y_back=back, turn=turns)
+    result = middle_y([values[n] for n in range(16)], tables, lane_roll)
     for n, value in enumerate(result):
         out[n] = value
 
 
-def backward_kernel(values, narrow, wide, out, one, two, flags):
-    fetch = Fetch()
-    fetch.start("x_back", rows_of(narrow, "x_back"), one, flags.at[0])
-    fetch.start("turn", rows_of(wide, "turn_x"), two, flags.at[1])
+def backward_kernel(values, table, turns, out):
     result = backward_x(
-        values[...].reshape(256, 128),
-        split_doubled(fetch.get("x_back")),
-        *split_pair(fetch.get("turn")),
-        lane_roll,
+        values[...].reshape(256, 128), split_doubled(table[...]), *split_pair(turns[...]), lane_roll
     )
     for n, value in enumerate(result):
         out[n] = value.astype(bf16)
 
 
-def last_kernel(values, velocity, table, out, kept, flags):
-    fetch = Fetch()
-    fetch.start("velocity", velocity, kept, flags.at[0])
+def last_kernel(values, velocity, table, out):
     loaded = [values[n].astype(f32) for n in range(32)]
     fields = [jnp.concatenate([v[4 * n : 4 * n + 4] for v in loaded], 0) for n in range(3)]
     plain, derived = split_pair(table[...])
     gradient = depth_back(fields, (split_pair(plain), split_pair(derived)))
-    velocity_before = fetch.get("velocity")
     for n, value in enumerate(gradient):
-        out[n] = velocity_before[n] - value
+        out[n] = velocity[n] - value
 
 
 def swap(modes, axis):
@@ -435,23 +426,24 @@
     return call(forward_kernel, shape, (modes, *tables))
 
 
-def solve_y(modes, narrow, wide):
+def solve_y(modes, wide):
     shape = jax.ShapeDtypeStruct((16, 16, 128), f32)
-    rows = [(512, bf16), (512, bf16), (48, f32), (8, f32), (8, f32)]
-    return fetching(middle_kernel, shape, (modes, narrow, wide), [near, far, far], rows)
-
-
-def from_x_modes(modes, narrow, wide):
+    tables = [table_rows(narrow_tables, name) for name in ("y", "y_back")]
+    tables.append(table_rows(wide_tables, "turn_y", "eigen_y"))
+    rows = [(8, f32), (8, f32)]
+    return fetching(middle_kernel, shape, (modes, *tables, wide), [near] * 4 + [far], rows)
+
+
+def from_x_modes(modes):
     shape = jax.ShapeDtypeStruct((32, 12, 128), bf16)
-    rows = [(512, bf16), (64, f32)]
-    return fetching(backward_kernel, shape, (modes, narrow, wide), [near, far, far], rows)
+    tables = (table_rows(narrow_tables, "x_back"), table_rows(wide_tables, "turn_x"))
+    return call(backward_kernel, shape, (modes, *tables))
 
 
 def from_depth_modes(modes, columns):
     shape = jax.ShapeDtypeStruct((3, 128, 128), f32)
     table = table_rows(narrow_tables, "depth", "depth_back_slope")
-    extra = [pltpu.VMEM((3, 128, 128), f32)]
-    return fetching(last_kernel, shape, (modes, columns, table), [near, far, near], [], extra)
+    return call(last_kernel, shape, (modes, columns, table))
 
 
 def pack_y_kernel(s_far, v_far, k_far, up, down, v, s, k, flags):
@@ -750,7 +742,7 @@
     k = diffusivity.reshape(128, 128)
     listed = burn_list.reshape(64)
     up, down, kept = pack_y(s, v, k)
-    narrow, wide = jnp.asarray(narrow_tables), jnp.asarray(wide_tables)
+    wide = jnp.asarray(wide_tables)
     network = (w_in, w_mid, w_out)
     strips = exchange(up, down, "gy")
     modes = to_depth_modes(kept.reshape(3, 128, 128))
@@ -762,10 +754,10 @@
     modes = swap(modes, "gy")
     moved = transport(s, v, k, strips, faces)
     modes, moved = after(modes, moved)
-    modes = swap(solve_y(modes, narrow, wide), "gy")
+    modes = swap(solve_y(modes, wide), "gy")
     moved = react(moved, listed, network, 0, early_slots)
     modes, moved = after(modes, moved)
-    modes = swap(from_x_modes(modes, narrow, wide), "gx")
+    modes = swap(from_x_modes(modes), "gx")
     moved = react(moved, listed, network, early_slots, 64)
     velocity_out = from_depth_modes(modes, velocity.reshape(3, 128, 128))
     return (moved.reshape(scalars.shape), velocity_out.reshape(velocity.shape))

time: 104 us -> 102 us (0.981)
  Pallas kernels: 34.7 us -> 32.6 us
    pallas_call x3 -> x1, Pallas kernels: 6.05 us -> 1.96 us  [fetching(): pl.pallas_call(body, out_shape=out_shape, in_specs=specs, scratch_shapes=...]
    pallas_call x2 -> x4, Pallas kernels: 2.04 us -> 4.09 us  [call(): pl.pallas_call(body, out_shape=out_shape, compiler_params=pltpu.CompilerP...]
  transfers between devices with their start and end apart: 8 -> 8, of which waited for: 5 -> 5; matrix products, arithmetic and copies ran while one was open for 0% -> 0% of each run, Pallas kernels for 24% -> 25%
where the time goes in v4:
time: 102 us; the launch traced here: 101 us
  starting transfers between devices  54.1 us (53%)
  Pallas kernels  32.6 us (32%)
  waiting for transfers between devices  13.4 us (13%)
    all_to_all x4, starting transfers between devices, swap(): return lax.all_to_all(modes, axis, split_axis=0, concat_axis=0, tiled=True)  38.6 us
    pallas_call x2, Pallas kernels, react(): pl.pallas_call(functools.partial(react_kernel, begin, end), out_shape=jax...  19.8 us
    ppermute x2, waiting for transfers between devices, exchange(): return (low, lax.ppermute(down, axis, [(b, a) for a, b in forward]))  8.84 us
    ppermute x2, starting transfers between devices, exchange(): return (low, lax.ppermute(down, axis, [(b, a) for a, b in forward]))  8.57 us
    ppermute x2, starting transfers between devices, exchange(): low = lax.ppermute(up, axis, forward)  6.95 us
    pallas_call x1, Pallas kernels, transport(): pl.pallas_call(transport_kernel, out_shape=jax.ShapeDtypeStruct((2560, 12...  5.06 us
    pallas_call x4, Pallas kernels, call(): pl.pallas_call(body, out_shape=out_shape, compiler_params=pltpu.CompilerP...  4.09 us
    ppermute x2, waiting for transfers between devices, exchange(): low = lax.ppermute(up, axis, forward)  3.05 us
  transfers between devices with their start and end apart: 8, of which 5 were waited for; matrix products, arithmetic and copies ran while one was open for 0% of the time, Pallas kernels for 25%

profile of v4, /device:TPU:1, one launch (start us, length us, event | category | flops | bytes accessed | tf_op | source)
XLA Modules:
  0.0 101.2 jit_solution(14877050170577303940)
XLA Ops:
  0.6 0.0 copy-start.6
  0.7 1.6 %pack_y.1 = (bf16[48,8,128]{2,1,0:T(8,128)(2,1)S(1)}, bf16[48,8,128]{2,1,0:T(8,128)(2,1)S(1)}, f32[384,128]{1,0:T(8,128)S(1)}) custom-call(f32[2560,128]{1,0:T(8,128)} %bitcast.9, f32[384,128]{1,0:T(8,128)} %bitcast.12, f32[128,128]{1,0:T(8,128)} %bitcast.16), custom_call_target="tpu_custom_call" | custom-call | tf_op jit(solution)/shard_map/pack_y/pallas_call | solution.py:675
  2.3 1.0 shard_map.176
  3.3 16.5 %all-to-all-start = ((bf16[32,12,128]{2,1,0:T(8,128)(2,1)}), bf16[32,12,128]{2,1,0:T(8,128)(2,1)S(1)}, u32[]{:S(2)}, u32[]{:S(2)}) async-start(bf16[32,12,128]{2,1,0:T(8,128)(2,1)} %shard_map.176), calls=%async_computation | async-start | bytes 262144 | tf_op jit(solution)/shard_map/all_to_all | solution.py:384
  19.8 4.0 %collective-permute-start = (bf16[48,8,128]{2,1,0:T(8,128)(2,1)S(1)}, bf16[48,8,128]{2,1,0:T(8,128)(2,1)S(1)}, u32[]{:S(2)}, u32[]{:S(2)}) collective-permute-start(bf16[48,8,128]{2,1,0:T(8,128)(2,1)S(1)} %get-tuple-element.13), channel_id=1, source_target_pairs={{0,1},{1,2},{2,3},{3,4},{4,5},{5,6},{6,7},{7,8},{8,9},{9,10},{10,1... | collective-permute-start | bytes 294920 | tf_op jit(solution)/shard_map/ppermute | solution.py:669
  23.8 1.9 %collective-permute-start.1 = (bf16[48,8,128]{2,1,0:T(8,128)(2,1)S(1)}, bf16[48,8,128]{2,1,0:T(8,128)(2,1)S(1)}, u32[]{:S(2)}, u32[]{:S(2)}) collective-permute-start(bf16[48,8,128]{2,1,0:T(8,128)(2,1)S(1)} %get-tuple-element.14), channel_id=1, source_target_pairs={{1,0},{2,1},{3,2},{4,3},{5,4},{6,5},{7,6},{8,7},{9,8},{10,9},{11,1... | collective-permute-start | bytes 294920 | tf_op jit(solution)/shard_map/ppermute | solution.py:670
  25.7 4.3 %collective-permute-done.1.yhigh = bf16[48,8,128]{2,1,0:T(8,128)(2,1)S(1)} collective-permute-done((bf16[48,8,128]{2,1,0:T(8,128)(2,1)S(1)}, bf16[48,8,128]{2,1,0:T(8,128)(2,1)S(1)}, u32[]{:S(2)}, u32[]{:S(2)}) %collective-permute-start.1) | collective-permute-done | bytes 98336 | tf_op jit(solution)/shard_map/ppermute | solution.py:670
  30.0 0.1 pack_x.1
  30.1 1.0 %all-to-all-done.values = bf16[32,12,128]{2,1,0:T(8,128)(2,1)S(1)} async-done(((bf16[32,12,128]{2,1,0:T(8,128)(2,1)}), bf16[32,12,128]{2,1,0:T(8,128)(2,1)S(1)}, u32[]{:S(2)}, u32[]{:S(2)}) %all-to-all-start) | async-done | bytes 98336 | tf_op jit(solution)/shard_map/all_to_all | solution.py:384
  31.2 1.0 %shard_map.177 = f32[16,16,128]{2,1,0:T(8,128)} custom-call(bf16[32,12,128]{2,1,0:T(8,128)(2,1)S(1)} %all-to-all-done.values, bf16[512,128]{1,0:T(8,128)(2,1)S(1)} %copy-done.8, f32[64,128]{1,0:T(8,128)S(1)} %copy-done.9), custom_call_target="tpu_custom_call" | custom-call | tf_op jit(solution)/shard_map/pallas_call | solution.py:276
  32.2 6.5 %all-to-all-start.1 = ((f32[16,16,128]{2,1,0:T(8,128)}), f32[16,16,128]{2,1,0:T(8,128)S(1)}, u32[]{:S(2)}, u32[]{:S(2)}) async-start(f32[16,16,128]{2,1,0:T(8,128)} %shard_map.177), calls=%async_computation.1 | async-start | bytes 262144 | tf_op jit(solution)/shard_map/all_to_all | solution.py:384
  38.7 3.0 %collective-permute-start.2 = (bf16[48,16,128]{2,1,0:T(8,128)(2,1)S(1)}, bf16[48,16,128]{2,1,0:T(8,128)(2,1)S(1)}, u32[]{:S(2)}, u32[]{:S(2)}) collective-permute-start(bf16[48,16,128]{2,1,0:T(8,128)(2,1)S(1)} %get-tuple-element.15), channel_id=1, source_target_pairs={{0,16},{16,32},{32,48},{48,64},{64,80},{80,96},{96,112},{112,128},... | collective-permute-start | bytes 589832 | tf_op jit(solution)/shard_map/ppermute | solution.py:669
  41.7 6.6 %collective-permute-start.3 = (bf16[48,16,128]{2,1,0:T(8,128)(2,1)S(1)}, bf16[48,16,128]{2,1,0:T(8,128)(2,1)S(1)}, u32[]{:S(2)}, u32[]{:S(2)}) collective-permute-start(bf16[48,16,128]{2,1,0:T(8,128)(2,1)S(1)} %get-tuple-element.16), channel_id=1, source_target_pairs={{16,0},{32,16},{48,32},{64,48},{80,64},{96,80},{112,96},{128,112},... | collective-permute-start | bytes 589832 | tf_op jit(solution)/shard_map/ppermute | solution.py:670
  48.4 3.1 %collective-permute-done.2.xlow = bf16[48,16,128]{2,1,0:T(8,128)(2,1)S(1)} collective-permute-done((bf16[48,16,128]{2,1,0:T(8,128)(2,1)S(1)}, bf16[48,16,128]{2,1,0:T(8,128)(2,1)S(1)}, u32[]{:S(2)}, u32[]{:S(2)}) %collective-permute-start.2) | collective-permute-done | bytes 196640 | tf_op jit(solution)/shard_map/ppermute | solution.py:669
  51.4 4.6 %collective-permute-done.3.xhigh = bf16[48,16,128]{2,1,0:T(8,128)(2,1)S(1)} collective-permute-done((bf16[48,16,128]{2,1,0:T(8,128)(2,1)S(1)}, bf16[48,16,128]{2,1,0:T(8,128)(2,1)S(1)}, u32[]{:S(2)}, u32[]{:S(2)}) %collective-permute-start.3) | collective-permute-done | bytes 196640 | tf_op jit(solution)/shard_map/ppermute | solution.py:670
  56.0 5.1 %transport.1.s = f32[2560,128]{1,0:T(8,128)S(1)} custom-call(f32[2560,128]{1,0:T(8,128)} %bitcast.10, f32[384,128]{1,0:T(8,128)S(1)} %bitcast.14, f32[128,128]{1,0:T(8,128)S(1)} %bitcast.18, bf16[48,8,128]{2,1,0:T(8,128)(2,1)S(1)} %collective-permute-done.ylow, bf16[48,8,128]{2,1,0:T(8,128)(2,1)S(1)} %collective-permute-done.1.yhigh, ...), custom_call_target="tpu_custom_call" | custom-call | tf_op jit(solution)/shard_map/transport/pallas_call | solution.py:702
  61.1 2.0 %shard_map.178 = f32[16,16,128]{2,1,0:T(8,128)} custom-call(f32[16,16,128]{2,1,0:T(8,128)S(1)} %all-to-all-done.1.values, bf16[512,128]{1,0:T(8,128)(2,1)S(1)} %copy-done.5, bf16[512,128]{1,0:T(8,128)(2,1)S(1)} %copy-done.4, f32[48,128]{1,0:T(8,128)S(1)} %copy-done.10, f32[496,128]{1,0:T(8,128)} %constant.18.clone.wide), custom_call_target="tpu_custom_call" | custom-call | tf_op jit(solution)/shard_map/pallas_call | solution.py:401
  63.0 6.1 %all-to-all-start.2 = ((f32[16,16,128]{2,1,0:T(8,128)}), f32[16,16,128]{2,1,0:T(8,128)S(1)}, u32[]{:S(2)}, u32[]{:S(2)}) async-start(f32[16,16,128]{2,1,0:T(8,128)} %shard_map.178), calls=%async_computation.2 | async-start | bytes 262144 | tf_op jit(solution)/shard_map/all_to_all | solution.py:384
  69.1 5.6 %react.2.s = f32[2560,128]{1,0:T(8,128)S(1)} custom-call(s32[64]{0:T(128)S(1)} %bitcast.20, f32[2560,128]{1,0:T(8,128)S(1)} %transport.1.s, bf16[20,800]{1,0:T(8,128)(2,1)} %bitcast.24, bf16[400,800]{1,0:T(8,128)(2,1)} %mid_far.3, bf16[20,400]{1,0:T(8,128)(2,1)} %out_far.3), custom_call_target="tpu_custom_call" | custom-call | tf_op jit(solution)/shard_map/react/pallas_call | solution.py:721
  74.7 0.5 all-to-all-done.2.values
  75.2 1.1 %shard_map.179 = bf16[32,12,128]{2,1,0:T(8,128)(2,1)} custom-call(f32[16,16,128]{2,1,0:T(8,128)S(1)} %all-to-all-done.2.values, bf16[512,128]{1,0:T(8,128)(2,1)S(1)} %copy-done.7, f32[64,128]{1,0:T(8,128)S(1)} %copy-done.9), custom_call_target="tpu_custom_call" | custom-call | tf_op jit(solution)/shard_map/pallas_call | solution.py:276
  76.3 9.6 %all-to-all-start.3 = ((bf16[32,12,128]{2,1,0:T(8,128)(2,1)}), bf16[32,12,128]{2,1,0:T(8,128)(2,1)S(1)}, u32[]{:S(2)}, u32[]{:S(2)}) async-start(bf16[32,12,128]{2,1,0:T(8,128)(2,1)} %shard_map.179), calls=%async_computation.3 | async-start | bytes 262144 | tf_op jit(solution)/shard_map/all_to_all | solution.py:384
  85.9 14.3 %react.3 = f32[2560,128]{1,0:T(8,128)} custom-call(s32[64]{0:T(128)S(1)} %bitcast.21, f32[2560,128]{1,0:T(8,128)S(1)} %react.2.s, bf16[20,800]{1,0:T(8,128)(2,1)} %bitcast.25, bf16[400,800]{1,0:T(8,128)(2,1)} %mid_far.3, bf16[20,400]{1,0:T(8,128)(2,1)} %out_far.3), custom_call_target="tpu_custom_call" | custom-call | tf_op jit(solution)/shard_map/react/pallas_call | solution.py:721
  100.2 1.0 shard_map.180
  (26 shorter events, 0.1 us)
Async XLA Ops:
  0.6 1.7 %copy-start.6 = (bf16[512,128]{1,0:T(8,128)(2,1)S(1)}, bf16[512,128]{1,0:T(8,128)(2,1)}, u32[]{:S(2)}) copy-start(bf16[512,128]{1,0:T(8,128)(2,1)} %constant.19.clone.table) | copy-start | bytes 393220
  0.6 29.4 %copy-start.1 = (f32[3,8,16,128]{3,2,1,0:T(8,128)S(1)}, f32[3,8,16,128]{3,2,1,0:T(8,128)}, u32[]{:S(2)}) copy-start(f32[3,8,16,128]{3,2,1,0:T(8,128)} %param.18) | copy-start | bytes 589828
  0.7 29.4 %copy-start.2 = (f32[8,16,128]{2,1,0:T(8,128)S(1)}, f32[8,16,128]{2,1,0:T(8,128)}, u32[]{:S(2)}) copy-start(f32[8,16,128]{2,1,0:T(8,128)} %param.19) | copy-start | bytes 196612
  0.7 29.4 %copy-start = (f32[20,8,16,128]{3,2,1,0:T(8,128)S(1)}, f32[20,8,16,128]{3,2,1,0:T(8,128)}, u32[]{:S(2)}) copy-start(f32[20,8,16,128]{3,2,1,0:T(8,128)} %param.17) | copy-start | bytes 3932164
  2.3 28.9 %copy-start.8 = (bf16[512,128]{1,0:T(8,128)(2,1)S(1)}, bf16[512,128]{1,0:T(8,128)(2,1)}, u32[]{:S(2)}) copy-start(bf16[512,128]{1,0:T(8,128)(2,1)} %constant.20.clone.table) | copy-start | bytes 393220
  2.3 28.9 %copy-start.9 = (f32[64,128]{1,0:T(8,128)S(1)}, f32[64,128]{1,0:T(8,128)}, u32[]{:S(2)}) copy-start(f32[64,128]{1,0:T(8,128)} %constant.21.clone.turns) | copy-start | bytes 98308
  3.3 27.8 %all-to-all-start = ((bf16[32,12,128]{2,1,0:T(8,128)(2,1)}), bf16[32,12,128]{2,1,0:T(8,128)(2,1)S(1)}, u32[]{:S(2)}, u32[]{:S(2)}) async-start(bf16[32,12,128]{2,1,0:T(8,128)(2,1)} %shard_map.176), calls=%async_computation | async-start | bytes 262144 | tf_op jit(solution)/shard_map/all_to_all | solution.py:384
  19.8 5.9 %collective-permute-start = (bf16[48,8,128]{2,1,0:T(8,128)(2,1)S(1)}, bf16[48,8,128]{2,1,0:T(8,128)(2,1)S(1)}, u32[]{:S(2)}, u32[]{:S(2)}) collective-permute-start(bf16[48,8,128]{2,1,0:T(8,128)(2,1)S(1)} %get-tuple-element.13), channel_id=1, source_target_pairs={{0,1},{1,2},{2,3},{3,4},{4,5},{5,6},{6,7},{7,8},{8,9},{9,10},{10,1... | collective-permute-start | bytes 294920 | tf_op jit(solution)/shard_map/ppermute | solution.py:669
  23.8 6.2 %collective-permute-start.1 = (bf16[48,8,128]{2,1,0:T(8,128)(2,1)S(1)}, bf16[48,8,128]{2,1,0:T(8,128)(2,1)S(1)}, u32[]{:S(2)}, u32[]{:S(2)}) collective-permute-start(bf16[48,8,128]{2,1,0:T(8,128)(2,1)S(1)} %get-tuple-element.14), channel_id=1, source_target_pairs={{1,0},{2,1},{3,2},{4,3},{5,4},{6,5},{7,6},{8,7},{9,8},{10,9},{11,1... | collective-permute-start | bytes 294920 | tf_op jit(solution)/shard_map/ppermute | solution.py:670
  32.2 28.8 %all-to-all-start.1 = ((f32[16,16,128]{2,1,0:T(8,128)}), f32[16,16,128]{2,1,0:T(8,128)S(1)}, u32[]{:S(2)}, u32[]{:S(2)}) async-start(f32[16,16,128]{2,1,0:T(8,128)} %shard_map.177), calls=%async_computation.1 | async-start | bytes 262144 | tf_op jit(solution)/shard_map/all_to_all | solution.py:384
  38.7 22.4 %copy-start.4 = (bf16[512,128]{1,0:T(8,128)(2,1)S(1)}, bf16[512,128]{1,0:T(8,128)(2,1)}, u32[]{:S(2)}) copy-start(bf16[512,128]{1,0:T(8,128)(2,1)} %constant.23.clone.back) | copy-start | bytes 393220
  38.7 22.4 %copy-start.5 = (bf16[512,128]{1,0:T(8,128)(2,1)S(1)}, bf16[512,128]{1,0:T(8,128)(2,1)}, u32[]{:S(2)}) copy-start(bf16[512,128]{1,0:T(8,128)(2,1)} %constant.22.clone.table) | copy-start | bytes 393220
  38.7 22.4 %copy-start.10 = (f32[48,128]{1,0:T(8,128)S(1)}, f32[48,128]{1,0:T(8,128)}, u32[]{:S(2)}) copy-start(f32[48,128]{1,0:T(8,128)} %constant.24.clone.turns) | copy-start | bytes 73732
  38.7 30.4 %copy-start.11 = (s32[1,1,64]{2,1,0:T(1,128)S(1)}, s32[1,1,64]{2,1,0:T(1,128)}, u32[]{:S(2)}) copy-start(s32[1,1,64]{2,1,0:T(1,128)} %param.20) | copy-start | bytes 772
  38.7 12.7 %collective-permute-start.2 = (bf16[48,16,128]{2,1,0:T(8,128)(2,1)S(1)}, bf16[48,16,128]{2,1,0:T(8,128)(2,1)S(1)}, u32[]{:S(2)}, u32[]{:S(2)}) collective-permute-start(bf16[48,16,128]{2,1,0:T(8,128)(2,1)S(1)} %get-tuple-element.15), channel_id=1, source_target_pairs={{0,16},{16,32},{32,48},{48,64},{64,80},{80,96},{96,112},{112,128},... | collective-permute-start | bytes 589832 | tf_op jit(solution)/shard_map/ppermute | solution.py:669
  41.7 14.3 %collective-permute-start.3 = (bf16[48,16,128]{2,1,0:T(8,128)(2,1)S(1)}, bf16[48,16,128]{2,1,0:T(8,128)(2,1)S(1)}, u32[]{:S(2)}, u32[]{:S(2)}) collective-permute-start(bf16[48,16,128]{2,1,0:T(8,128)(2,1)S(1)} %get-tuple-element.16), channel_id=1, source_target_pairs={{16,0},{32,16},{48,32},{64,48},{80,64},{96,80},{112,96},{128,112},... | collective-permute-start | bytes 589832 | tf_op jit(solution)/shard_map/ppermute | solution.py:670
  63.0 12.2 %all-to-all-start.2 = ((f32[16,16,128]{2,1,0:T(8,128)}), f32[16,16,128]{2,1,0:T(8,128)S(1)}, u32[]{:S(2)}, u32[]{:S(2)}) async-start(f32[16,16,128]{2,1,0:T(8,128)} %shard_map.178), calls=%async_computation.2 | async-start | bytes 262144 | tf_op jit(solution)/shard_map/all_to_all | solution.py:384
  69.1 6.1 %copy-start.7 = (bf16[512,128]{1,0:T(8,128)(2,1)S(1)}, bf16[512,128]{1,0:T(8,128)(2,1)}, u32[]{:S(2)}) copy-start(bf16[512,128]{1,0:T(8,128)(2,1)} %constant.25.clone.table) | copy-start | bytes 393220
  76.3 23.9 %all-to-all-start.3 = ((bf16[32,12,128]{2,1,0:T(8,128)(2,1)}), bf16[32,12,128]{2,1,0:T(8,128)(2,1)S(1)}, u32[]{:S(2)}, u32[]{:S(2)}) async-start(bf16[32,12,128]{2,1,0:T(8,128)(2,1)} %shard_map.179), calls=%async_computation.3 | async-start | bytes 262144 | tf_op jit(solution)/shard_map/all_to_all | solution.py:384
  85.9 14.3 %copy-start.3 = (bf16[512,128]{1,0:T(8,128)(2,1)S(1)}, bf16[512,128]{1,0:T(8,128)(2,1)}, u32[]{:S(2)}) copy-start(bf16[512,128]{1,0:T(8,128)(2,1)} %constant.26.clone.table) | copy-start | bytes 393220
